TPU v7x, 32 devices: a whole 2x2x4 slice. The times are simulated.
32 devices in a mesh: bx: 4 (over z), by: 2 (over x), bz: 4 (over y, core).
Axes of the slice: x: 2, y: 2, z: 4, core: 2. Of those that a mesh axis runs over, the one named last changes fastest.
Arguments:
- estimate: float32 [64, 32, 512], P('bx', 'by', 'bz'), may hold values from 0.2 to 5
- observed: float32 [8, 64, 32, 512], P(None, 'bx', 'by', 'bz'), may hold values from 0.3 to 180, as said below
- coverage: int32 [8, 4, 2, 4], P(None, 'bx', 'by', 'bz'), may hold values from 0 to 1, as said below
- psf_taps: float32 [8, 3, 17], replicated, may hold values from 0.05 to 1
Outputs:
- refined: float32 [64, 32, 512], P('bx', 'by', 'bz')
Inputs may be any that keep to these rules, and one draw needn't show every extreme that they name: `coverage`: each block is covered by 2 to 8 views; in every draw some block is covered by all 8. `observed`: positive.
All inputs are finite; a program needn't handle non-finite values.
Results may differ from a plain program's by a relative error of at most 0.0001.
Values sent between devices are 32-bit elements; how exact they have to be, the bound alone decides.
A program may use at most 64 MiB of HBM per device.

v0:
```python
import functools

import jax
import jax.numpy as jnp
from jax import lax
from jax.experimental import pallas as pl
from jax.experimental.pallas import tpu as pltpu
from jax.sharding import PartitionSpec as P

F32 = jnp.float32
BF16 = jnp.bfloat16
MESH = pl.DeviceIdType.MESH


def split(values):
    high = values.astype(BF16)
    low = (values - high.astype(F32)).astype(BF16)
    return high, low


def dot(left, right, dims=((1,), (0,))):
    return lax.dot_general(left, right, (dims, ((), ())), preferred_element_type=F32)


def folded(values):
    half = values.shape[1] // 2
    return values[:, :half] + values[:, half:]


def rings(sizes):
    offsets = [(i, j, k) for i in range(sizes[0]) for j in range(sizes[1]) for k in range(sizes[2])]
    offsets = offsets[1:]
    if len(offsets) < 64:
        return offsets, offsets, []
    return (
        offsets,
        [offset for offset in offsets if offset[0] == 0],
        [offset for offset in offsets if offset[1:] == (0, 0)],
    )


def kernel(
    sizes,
    taps_ref,
    cover_ref,
    est_ref,
    obs_hbm,
    out_ref,
    obs,
    ext,
    ext_hi,
    ext_lo,
    pack,
    from_left,
    from_right,
    weight,
    weight_xy,
    weight_left,
    weight_right,
    scale,
    band,
    twin,
    gath_hi,
    gath_lo,
    scat,
    lined,
    spread,
    total,
    fringe,
    back_pack,
    back_left,
    back_right,
    back_xy,
    stat,
    stat_a,
    stat_b,
    part_a,
    obs_sem,
    out_send,
    out_recv,
    back_send,
    back_recv,
    a_send,
    a_recv,
    b_send,
    b_recv,
):
    n_x, n_y, n_z = sizes
    views, rows, cols, lanes = obs.shape
    length = taps_ref.shape[2]
    rad = (length - 1) // 2
    wide_x, wide_y = rows + 2 * rad, cols + 2 * rad
    groups = wide_x // 8
    me_x, me_y, me_z = lax.axis_index("bx"), lax.axis_index("by"), lax.axis_index("bz")

    fetch = pltpu.make_async_copy(obs_hbm, obs, obs_sem)
    fetch.start()

    def exists(dx, dy, dz):
        ok = None
        for step, me, count in ((dx, me_x, n_x), (dy, me_y, n_y), (dz, me_z, n_z)):
            if step == 0:
                continue
            inside = (me + step >= 0) & (me + step < count)
            ok = inside if ok is None else ok & inside
        return ok

    def device(dx, dy, dz):
        return {"bx": me_x + dx, "by": me_y + dy, "bz": me_z + dz}

    steps = (-1, 0, 1)
    around = [(dx, dy, dz) for dz in steps for dx in steps for dy in steps if (dx, dy, dz) != (0, 0, 0)]
    ring_all, ring_a, ring_b = rings(sizes)

    def partner(i, j, k):
        return {
            "bx": lax.rem(me_x + i, n_x),
            "by": lax.rem(me_y + j, n_y),
            "bz": lax.rem(me_z + k, n_z),
        }

    ext[...] = jnp.zeros(ext.shape, F32)
    ext[rad : rad + rows, rad : rad + cols, :] = est_ref[...]
    from_left[...] = jnp.zeros(from_left.shape, F32)
    from_right[...] = jnp.zeros(from_right.shape, F32)
    weight_xy[...] = jnp.zeros(weight_xy.shape, F32)
    weight_left[...] = jnp.zeros(weight_left.shape, F32)
    weight_right[...] = jnp.zeros(weight_right.shape, F32)
    back_xy[...] = jnp.zeros(back_xy.shape, F32)
    back_left[...] = jnp.zeros(back_left.shape, F32)
    back_right[...] = jnp.zeros(back_right.shape, F32)
    for v in range(views):
        row = jnp.full((1, lanes), cover_ref[v], jnp.int32).astype(F32)
        weight[v : v + 1, :] = row
        weight_xy[1, 1, v : v + 1, :] = row

    barrier = pltpu.get_barrier_semaphore()
    for offset in ring_all:
        pl.semaphore_signal(barrier, inc=1, device_id=partner(*offset), device_id_type=MESH)

    lane = lax.broadcasted_iota(jnp.int32, (cols, lanes), 1)
    for g in range(rows // 8):
        merged = jnp.zeros((cols, lanes), F32)
        for i in range(8):
            rolled = pltpu.roll(est_ref[8 * g + i], 2 * rad * i + rad, 1)
            merged = jnp.where(lane // (2 * rad) == i, rolled, merged)
        pack[g] = merged

    def cut(step, size, width):
        return pl.ds(0, size) if step == 0 else pl.ds(0 if step < 0 else size - width, width)

    def wide(step, size, width):
        return pl.ds(width, size) if step == 0 else pl.ds(0 if step < 0 else width + size, width)

    pack_rows, pack_rad = rows // 8, rad // 8

    def out_copies():
        for slot, (dx, dy, dz) in enumerate(around):
            size, width = (rows, rad) if dz == 0 else (pack_rows, pack_rad)
            source = est_ref if dz == 0 else pack
            target = (from_right, ext, from_left)[dz + 1]
            weights = (weight_right, weight_xy, weight_left)[dz + 1]
            pairs = (
                (
                    source.at[cut(dx, size, width), cut(dy, cols, rad), :],
                    target.at[wide(-dx, size, width), wide(-dy, cols, rad), :],
                ),
                (weight, weights.at[1 - dx, 1 - dy]),
            )
            copies = [
                pltpu.make_async_remote_copy(
                    src_ref=pair[0],
                    dst_ref=pair[1],
                    send_sem=out_send.at[slot, which],
                    recv_sem=out_recv.at[slot, which],
                    device_id=device(dx, dy, dz),
                    device_id_type=MESH,
                )
                for which, pair in enumerate(pairs)
            ]
            yield exists(dx, dy, dz), exists(-dx, -dy, -dz), copies

    def back_copies():
        for slot, (dx, dy, dz) in enumerate(around):
            size, width = (rows, rad) if dz == 0 else (pack_rows, pack_rad)
            source = total if dz == 0 else back_pack
            target = (back_right, back_xy, back_left)[dz + 1]
            copy = pltpu.make_async_remote_copy(
                src_ref=source.at[wide(dx, size, width), wide(dy, cols, rad), :],
                dst_ref=target.at[wide(-dx, size, width), wide(-dy, cols, rad), :],
                send_sem=back_send.at[slot],
                recv_sem=back_recv.at[slot],
                device_id=device(dx, dy, dz),
                device_id_type=MESH,
            )
            yield exists(dx, dy, dz), exists(-dx, -dy, -dz), [copy]

    def start(family):
        for sends, _, copies in family():

            @pl.when(sends)
            def _():
                for copy in copies:
                    copy.start()

    def arrive(family):
        for _, takes, copies in family():

            @pl.when(takes)
            def _():
                for copy in copies:
                    copy.wait_recv()

    def leave(family):
        for sends, _, copies in family():

            @pl.when(sends)
            def _():
                for copy in copies:
                    copy.wait_send()

    def build(v, carry):
        def summed(dim):
            values = [taps_ref[dim, v, k] for k in range(length)]
            while len(values) > 1:
                values = [sum(values[i : i + 2]) for i in range(0, len(values), 2)]
            return jnp.full((8, lanes), values[0], F32)

        inverse = 1.0 / (summed(0) * summed(1) * summed(2))

        def chosen(offset, dim):
            result = jnp.zeros(offset.shape, F32)
            for k in range(length):
                result = jnp.where(offset == k, taps_ref[dim, v, k], result)
            return result

        def iota(shape, dim):
            return lax.broadcasted_iota(jnp.int32, shape, dim)

        shape = (lanes, lanes)
        main = chosen(iota(shape, 0) - iota(shape, 1) + rad, 2)
        shape = (2 * rad, lanes)
        row, col = iota(shape, 0), iota(shape, 1)
        edge = chosen(jnp.where(row < rad, row, row + lanes) - col, 2)
        for first, part in ((0, main), (lanes, edge)):
            part = (part.reshape(-1, 8, lanes) * inverse[None]).reshape(part.shape)
            high, low = split(part)
            band[v, first : first + part.shape[0], :] = jnp.concatenate([high, low], axis=1)
            twin[v, first : first + part.shape[0], :] = jnp.concatenate([high, high], axis=1)
        rest = band.shape[1] - lanes - 2 * rad
        band[v, lanes + 2 * rad :, :] = jnp.zeros((rest, 2 * lanes), BF16)
        twin[v, lanes + 2 * rad :, :] = jnp.zeros((rest, 2 * lanes), BF16)
        shape = (8 * cols, 8 * wide_y)
        row, col = iota(shape, 0), iota(shape, 1)
        offset = jnp.where(row // cols == col // wide_y, col % wide_y - row % cols, -1)
        high, low = split(chosen(offset, 1))
        gath_hi[v], gath_lo[v] = high, low
        shape = (8 * wide_y, 8 * cols)
        row, col = iota(shape, 0), iota(shape, 1)
        offset = jnp.where(row // wide_y == col // cols, row % wide_y - col % cols, -1)
        high, low = split(chosen(offset, 1))
        scat[v] = jnp.concatenate([high, low], axis=1)
        return carry

    early = min(3, views)
    lax.fori_loop(0, early, build, 0)
    pl.semaphore_wait(barrier, len(ring_all))
    start(out_copies)
    lax.fori_loop(early, views, build, 0)

    fetch.wait()
    count = jnp.zeros((1, lanes), F32)
    seen = jnp.zeros((8, lanes), F32)
    for v in range(views):
        count = count + weight[v : v + 1, :]
        seen = seen + weight[v : v + 1, :] * jnp.sum(obs[v].reshape(-1, 8, lanes), axis=0)
    stat[0:1] = jnp.sum(seen / count, axis=0, keepdims=True)

    arrive(out_copies)
    lane = lax.broadcasted_iota(jnp.int32, (wide_y, lanes), 1)
    high, low = split(ext[...].reshape(wide_x * wide_y, lanes))
    ext_hi[:, :lanes] = high
    ext_lo[:, :lanes] = low
    for g in range(groups):
        merged = jnp.where(lane % (2 * rad) < rad, from_left[g], from_right[g])
        for i in range(8):
            shift = (lanes - 2 * rad * i) % lanes
            rolled = pltpu.roll(merged, shift, 1) if shift else merged
            high, low = split(rolled)
            first = (8 * g + i) * wide_y
            ext_hi[first : first + wide_y, lanes:] = high
            ext_lo[first : first + wide_y, lanes:] = low

    thin = lax.broadcasted_iota(jnp.int32, (rad, lanes), 1)
    for v in range(views):
        for dx in range(3):
            for dy in range(3):
                mid = jnp.broadcast_to(weight_xy[dx, dy, v : v + 1, :], (rad, lanes))
                left = jnp.broadcast_to(weight_left[dx, dy, v : v + 1, :], (rad, lanes))
                right = jnp.broadcast_to(weight_right[dx, dy, v : v + 1, :], (rad, lanes))
                side = jnp.where(thin < rad, left, jnp.where(thin < 2 * rad, right, 0.0))
                for first in range(0 if dy == 0 else (rad if dy == 1 else rad + cols), rad if dy == 0 else (rad + cols if dy == 1 else wide_y), rad):
                    scale[v, dx, first : first + rad, :lanes] = mid
                    scale[v, dx, first : first + rad, lanes:] = side

    total[...] = jnp.zeros(total.shape, F32)
    fringe[...] = jnp.zeros(fringe.shape, F32)

    def one_view(v, carry):
        size = 8 * wide_y
        high_part = slice(0, lanes)
        for g in range(groups):
            here = slice(g * size, (g + 1) * size)
            blurred = folded(dot(ext_hi[here, :], band[v])) + dot(ext_lo[here, :], band[v, :, high_part])
            high, low = split(blurred)
            line = folded(dot(gath_hi[v], jnp.concatenate([high, low], axis=1))) + dot(gath_lo[v], high)
            lined[8 * g : 8 * g + 8] = line.reshape(8, cols, lanes)
        blur = taps_ref[0, v, 0] * lined[0:rows]
        for k in range(1, length):
            blur = blur + taps_ref[0, v, k] * lined[k : k + rows]
        spread[...] = obs[v] / blur
        for g in range(groups):
            pieces = []
            for e in range(8 * g, 8 * g + 8):
                piece = None
                for a in range(rows):
                    if 0 <= e - a < length:
                        term = taps_ref[0, v, e - a] * spread[a]
                        piece = term if piece is None else piece + term
                pieces.append(piece)
            piece = jnp.concatenate(pieces, axis=0)
            both = jnp.concatenate(split(piece), axis=1)
            piece = folded(dot(scat[v], jnp.concatenate([both, both], axis=0)))
            high, low = split(piece)
            flip = ((1,), (1,))
            piece = dot(jnp.concatenate([high, low], axis=1), twin[v], flip)
            piece = piece + dot(high, band[v, :, lanes:], flip)
            piece = piece.reshape(8, wide_y, 2 * lanes)
            dx = 0 if 8 * g < rad else (1 if 8 * g < rad + rows else 2)
            piece = piece * scale[v, dx][None]
            total[8 * g : 8 * g + 8] += piece[:, :, :lanes]
            fringe[8 * g : 8 * g + 8] += piece[:, :, lanes:]
        return carry

    lax.fori_loop(0, views, one_view, 0, unroll=2)

    for g in range(groups):
        merged = fringe[8 * g]
        for i in range(1, 8):
            merged = merged + pltpu.roll(fringe[8 * g + i], 2 * rad * i, 1)
        back_pack[g] = merged
    start(back_copies)
    arrive(back_copies)
    near = back_xy[...]

    def fold(values, size, rad, axis):
        low = lax.slice_in_dim(values, 0, rad, axis=axis)
        mid = lax.slice_in_dim(values, rad, rad + size, axis=axis)
        top = lax.slice_in_dim(values, rad + size, 2 * rad + size, axis=axis)
        if size == 2 * rad:
            return mid + jnp.concatenate([low, top], axis=axis)
        gap_shape = list(low.shape)
        gap_shape[axis] = size - rad
        gap = jnp.zeros(gap_shape, F32)
        return mid + jnp.concatenate([low, gap], axis=axis) + jnp.concatenate([gap, top], axis=axis)

    near = fold(fold(near, rows, rad, 0), cols, rad, 1)
    ends = jnp.where((lane % (2 * rad) < rad)[None], back_right[...], back_left[...])
    ends = fold(fold(ends, pack_rows, pack_rad, 0), cols, rad, 1)
    lane = lax.broadcasted_iota(jnp.int32, (cols, lanes), 1)
    outer = (lane < rad) | (lane >= lanes - rad)
    seen = jnp.zeros((8, lanes), F32)
    for x in range(rows):
        rolled = pltpu.roll(ends[x // 8], lanes - (2 * rad * (x % 8) + rad), 1)
        summed = total[rad + x, rad : rad + cols, :] + near[x] + jnp.where(outer, rolled, 0.0)
        updated = est_ref[x] * (summed / count)
        out_ref[x] = updated
        seen = seen + jnp.sum(updated.reshape(-1, 8, lanes), axis=0)
    stat[1:2] = jnp.sum(seen, axis=0, keepdims=True)

    def sums_a():
        for slot, offset in enumerate(ring_a):
            yield pltpu.make_async_remote_copy(
                src_ref=stat,
                dst_ref=stat_a.at[slot],
                send_sem=a_send.at[slot],
                recv_sem=a_recv.at[slot],
                device_id=partner(*offset),
                device_id_type=MESH,
            )

    def sums_b():
        for slot, offset in enumerate(ring_b):
            yield pltpu.make_async_remote_copy(
                src_ref=part_a,
                dst_ref=stat_b.at[slot],
                send_sem=b_send.at[slot],
                recv_sem=b_recv.at[slot],
                device_id=partner(*offset),
                device_id_type=MESH,
            )

    for copy in sums_a():
        copy.start()
    for copy in sums_a():
        copy.wait_recv()
    everything = stat[...] + jnp.sum(stat_a[...], axis=0)
    if ring_b:
        part_a[...] = everything
        for copy in sums_b():
            copy.start()
        for copy in sums_b():
            copy.wait_recv()
        everything = part_a[...] + jnp.sum(stat_b[...], axis=0)
    wanted = jnp.sum(everything[0:1], axis=1, keepdims=True)
    gotten = jnp.sum(everything[1:2], axis=1, keepdims=True)
    factor = jnp.broadcast_to(wanted, (1, lanes)) / jnp.broadcast_to(gotten, (1, lanes))
    out_ref[...] = out_ref[...] * factor.reshape(1, 1, lanes)

    for family in (out_copies, back_copies):
        leave(family)
    for copy in sums_a():
        copy.wait_send()
    for copy in sums_b():
        copy.wait_send()


def on_device(sizes, estimate, observed, coverage, psf_taps):
    rows, cols, lanes = estimate.shape
    views = observed.shape[0]
    rad = (psf_taps.shape[2] - 1) // 2
    wide_x, wide_y = rows + 2 * rad, cols + 2 * rad
    groups = wide_x // 8
    _, ring_a, ring_b = rings(sizes)
    n_a, n_b = len(ring_a), max(1, len(ring_b))

    def vm(*shape, dtype=F32):
        return pltpu.VMEM(shape, dtype)

    def dma(*shape):
        return pltpu.SemaphoreType.DMA(shape)

    scratch = [
        vm(*observed.shape),
        vm(wide_x, wide_y, lanes),
        vm(wide_x * wide_y, 2 * lanes, dtype=BF16),
        vm(wide_x * wide_y, 2 * lanes, dtype=BF16),
        vm(rows // 8, cols, lanes),
        vm(groups, wide_y, lanes),
        vm(groups, wide_y, lanes),
        vm(views, lanes),
        vm(3, 3, views, lanes),
        vm(3, 3, views, lanes),
        vm(3, 3, views, lanes),
        vm(views, 3, wide_y, 2 * lanes),
        vm(views, 2 * lanes, 2 * lanes, dtype=BF16),
        vm(views, 2 * lanes, 2 * lanes, dtype=BF16),
        vm(views, 8 * cols, 8 * wide_y, dtype=BF16),
        vm(views, 8 * cols, 8 * wide_y, dtype=BF16),
        vm(views, 8 * wide_y, 16 * cols, dtype=BF16),
        vm(wide_x, cols, lanes),
        vm(rows, cols, lanes),
        vm(wide_x, wide_y, lanes),
        vm(wide_x, wide_y, lanes),
        vm(groups, wide_y, lanes),
        vm(groups, wide_y, lanes),
        vm(groups, wide_y, lanes),
        vm(wide_x, wide_y, lanes),
        vm(2, lanes),
        vm(n_a, 2, lanes),
        vm(n_b, 2, lanes),
        vm(2, lanes),
        pltpu.SemaphoreType.DMA,
        dma(26, 2),
        dma(26, 2),
        dma(26),
        dma(26),
        dma(n_a),
        dma(n_a),
        dma(n_b),
        dma(n_b),
    ]
    return pl.pallas_call(
        functools.partial(kernel, sizes),
        out_shape=jax.ShapeDtypeStruct(estimate.shape, F32),
        in_specs=[
            pl.BlockSpec(memory_space=pltpu.SMEM),
            pl.BlockSpec(memory_space=pltpu.SMEM),
            pl.BlockSpec(memory_space=pltpu.VMEM),
            pl.BlockSpec(memory_space=pl.ANY),
        ],
        out_specs=pl.BlockSpec(memory_space=pltpu.VMEM),
        scratch_shapes=scratch,
        compiler_params=pltpu.CompilerParams(collective_id=0, has_side_effects=True),
    )(jnp.transpose(psf_taps, (1, 0, 2)), coverage.reshape(views), estimate, observed)


def solution(mesh):
    sizes = tuple(mesh.shape[axis] for axis in ("bx", "by", "bz"))
    return jax.shard_map(
        functools.partial(on_device, sizes),
        mesh=mesh,
        in_specs=(P("bx", "by", "bz"), P(None, "bx", "by", "bz"), P(None, "bx", "by", "bz"), P()),
        out_specs=P("bx", "by", "bz"),
        check_vma=False,
    )
```

profile of v0, /device:TPU:0, one launch (start us, length us, event | category | flops | bytes accessed | tf_op | source)
XLA Modules:
  0.0 40.9 jit_solution(7487917990581436118)
XLA Ops:
  0.0 39.3 %shard_map.46 = f32[16,16,128]{2,1,0:T(8,128)} custom-call(f32[3,8,17]{2,1,0:T(8,128)} %bitcast.2, s32[8]{0:T(128)} %bitcast.3, f32[16,16,128]{2,1,0:T(8,128)} %est_ref.1, f32[8,16,16,128]{3,2,1,0:T(8,128)} %obs_hbm.1), custom_call_target="tpu_custom_call" | custom-call | tf_op jit(solution)/shard_map/pallas_call | solution.py:483
  39.3 1.6 %copy.6 = f32[16,16,128]{2,1,0:T(8,128)} copy(f32[16,16,128]{2,1,0:T(8,128)} %shard_map.46) | data formatting | bytes 262144
where the time goes:
time: 41.1 us; the launch traced here: 40.9 us
  Pallas kernels  39.3 us (96%)
  local copies, waits for them, and re-layouts  1.57 us (4%)
    pallas_call x1, Pallas kernels, on_device(): pl.pallas_call(functools.partial(kernel, sizes), out_shape=jax.ShapeDtype...  39.3 us
    unnamed x1, local copies, waits for them, and re-layouts  1.57 us

commit v1 on v0

--- a/solution.py
+++ b/solution.py
@@ -41,11 +41,13 @@
 
 def kernel(
     sizes,
+    taps_hbm,
+    cover_hbm,
+    est_hbm,
+    obs_hbm,
+    out_ref,
     taps_ref,
     cover_ref,
-    est_ref,
-    obs_hbm,
-    out_ref,
     obs,
     ext,
     ext_hi,
@@ -53,11 +55,10 @@
     pack,
     from_left,
     from_right,
+    edge,
     weight,
-    weight_xy,
-    weight_left,
-    weight_right,
     scale,
+    inverses,
     band,
     twin,
     gath_hi,
@@ -75,7 +76,8 @@
     stat_a,
     stat_b,
     part_a,
-    obs_sem,
+    fetch_sem,
+    hop_sem,
     out_send,
     out_recv,
     back_send,
@@ -93,8 +95,16 @@
     groups = wide_x // 8
     me_x, me_y, me_z = lax.axis_index("bx"), lax.axis_index("by"), lax.axis_index("bz")
 
-    fetch = pltpu.make_async_copy(obs_hbm, obs, obs_sem)
-    fetch.start()
+    own_x, own_y = slice(rad, rad + rows), slice(rad, rad + cols)
+    own = ext.at[own_x, own_y, :]
+    loads = [
+        pltpu.make_async_copy(source, target, fetch_sem.at[which])
+        for which, (source, target) in enumerate(
+            ((est_hbm, own), (cover_hbm, cover_ref), (taps_hbm, taps_ref), (obs_hbm, obs))
+        )
+    ]
+    for load in loads:
+        load.start()
 
     def exists(dx, dy, dz):
         ok = None
@@ -119,30 +129,54 @@
             "bz": lax.rem(me_z + k, n_z),
         }
 
-    ext[...] = jnp.zeros(ext.shape, F32)
-    ext[rad : rad + rows, rad : rad + cols, :] = est_ref[...]
+    for part in ((slice(0, rad), slice(0, wide_y)), (slice(rad + rows, wide_x), slice(0, wide_y))):
+        ext[part[0], part[1], :] = jnp.zeros((rad, wide_y, lanes), F32)
+    for part in (slice(0, rad), slice(rad + cols, wide_y)):
+        ext[own_x, part, :] = jnp.zeros((rows, rad, lanes), F32)
     from_left[...] = jnp.zeros(from_left.shape, F32)
     from_right[...] = jnp.zeros(from_right.shape, F32)
-    weight_xy[...] = jnp.zeros(weight_xy.shape, F32)
-    weight_left[...] = jnp.zeros(weight_left.shape, F32)
-    weight_right[...] = jnp.zeros(weight_right.shape, F32)
+    weight[...] = jnp.zeros(weight.shape, F32)
+
+    barrier = pltpu.get_barrier_semaphore()
+    faces = [offset for offset in around if sum(map(abs, offset)) == 1]
+    near_by = sum(exists(*offset).astype(jnp.int32) for offset in faces)
+    rounds = n_x + n_y + n_z - 3
+
+    def greet(which):
+        semaphore = barrier if which == 0 else hop_sem.at[which - 1]
+        for offset in faces:
+
+            @pl.when(exists(*offset))
+            def _():
+                pl.semaphore_signal(semaphore, inc=1, device_id=device(*offset), device_id_type=MESH)
+
+    def meet(which):
+        pl.semaphore_wait(barrier if which == 0 else hop_sem.at[which - 1], near_by)
+        if which + 1 < rounds:
+            greet(which + 1)
+
+    greet(0)
+
     back_xy[...] = jnp.zeros(back_xy.shape, F32)
     back_left[...] = jnp.zeros(back_left.shape, F32)
     back_right[...] = jnp.zeros(back_right.shape, F32)
+    total[...] = jnp.zeros(total.shape, F32)
+    fringe[...] = jnp.zeros(fringe.shape, F32)
+
+    loads[1].wait()
+    lane = lax.broadcasted_iota(jnp.int32, (1, lanes), 1)
+    row = jnp.zeros((1, lanes), F32)
     for v in range(views):
-        row = jnp.full((1, lanes), cover_ref[v], jnp.int32).astype(F32)
-        weight[v : v + 1, :] = row
-        weight_xy[1, 1, v : v + 1, :] = row
-
-    barrier = pltpu.get_barrier_semaphore()
-    for offset in ring_all:
-        pl.semaphore_signal(barrier, inc=1, device_id=partner(*offset), device_id_type=MESH)
+        mine = jnp.full((1, lanes), cover_ref[v], jnp.int32).astype(F32)
+        row = jnp.where(lane // (lanes // views) == v, mine, row)
+    weight[13] = row
+    loads[0].wait()
 
     lane = lax.broadcasted_iota(jnp.int32, (cols, lanes), 1)
     for g in range(rows // 8):
         merged = jnp.zeros((cols, lanes), F32)
         for i in range(8):
-            rolled = pltpu.roll(est_ref[8 * g + i], 2 * rad * i + rad, 1)
+            rolled = pltpu.roll(ext[rad + 8 * g + i, own_y, :], 2 * rad * i + rad, 1)
             merged = jnp.where(lane // (2 * rad) == i, rolled, merged)
         pack[g] = merged
 
@@ -154,18 +188,23 @@
 
     pack_rows, pack_rad = rows // 8, rad // 8
 
-    def out_copies():
-        for slot, (dx, dy, dz) in enumerate(around):
+    def slot_of(dx, dy, dz):
+        return 9 * (dz + 1) + 3 * (dx + 1) + dy + 1
+
+    def out_copies(hops):
+        for dx, dy, dz in sorted(around, key=lambda offset: abs(offset[2])):
+            if sum(map(abs, (dx, dy, dz))) not in hops:
+                continue
+            slot = slot_of(dx, dy, dz)
             size, width = (rows, rad) if dz == 0 else (pack_rows, pack_rad)
-            source = est_ref if dz == 0 else pack
+            source = own if dz == 0 else pack
             target = (from_right, ext, from_left)[dz + 1]
-            weights = (weight_right, weight_xy, weight_left)[dz + 1]
             pairs = (
+                (weight.at[13], weight.at[slot_of(-dx, -dy, -dz)]),
                 (
                     source.at[cut(dx, size, width), cut(dy, cols, rad), :],
                     target.at[wide(-dx, size, width), wide(-dy, cols, rad), :],
                 ),
-                (weight, weights.at[1 - dx, 1 - dy]),
             )
             copies = [
                 pltpu.make_async_remote_copy(
@@ -181,7 +220,8 @@
             yield exists(dx, dy, dz), exists(-dx, -dy, -dz), copies
 
     def back_copies():
-        for slot, (dx, dy, dz) in enumerate(around):
+        for dx, dy, dz in sorted(around, key=lambda offset: abs(offset[2])):
+            slot = slot_of(dx, dy, dz)
             size, width = (rows, rad) if dz == 0 else (pack_rows, pack_rad)
             source = total if dz == 0 else back_pack
             target = (back_right, back_xy, back_left)[dz + 1]
@@ -196,7 +236,7 @@
             yield exists(dx, dy, dz), exists(-dx, -dy, -dz), [copy]
 
     def start(family):
-        for sends, _, copies in family():
+        for sends, _, copies in family:
 
             @pl.when(sends)
             def _():
@@ -204,7 +244,7 @@
                     copy.start()
 
     def arrive(family):
-        for _, takes, copies in family():
+        for _, takes, copies in family:
 
             @pl.when(takes)
             def _():
@@ -212,7 +252,7 @@
                     copy.wait_recv()
 
     def leave(family):
-        for sends, _, copies in family():
+        for sends, _, copies in family:
 
             @pl.when(sends)
             def _():
@@ -262,27 +302,42 @@
         scat[v] = jnp.concatenate([high, low], axis=1)
         return carry
 
-    early = min(3, views)
-    lax.fori_loop(0, early, build, 0)
-    pl.semaphore_wait(barrier, len(ring_all))
-    start(out_copies)
-    lax.fori_loop(early, views, build, 0)
-
-    fetch.wait()
-    count = jnp.zeros((1, lanes), F32)
+    meet(0)
+    start(out_copies((1,)))
+    loads[2].wait()
+    stops = [min(stop, views) for stop in (0, 2, 4, 6, views)]
+    for hop in range(1, 5):
+        lax.fori_loop(stops[hop - 1], stops[hop], build, 0)
+        if hop < rounds:
+            meet(hop)
+        if hop in (1, 2):
+            start(out_copies((hop + 1,)))
+
+    loads[3].wait()
+    def weight_of(rows_of, v):
+        first = v * (lanes // views)
+        return jnp.broadcast_to(rows_of[:, first : first + 1], rows_of.shape)
+
+    mine = jnp.broadcast_to(weight[13], (8, lanes))
+    count = jnp.zeros((8, lanes), F32)
     seen = jnp.zeros((8, lanes), F32)
     for v in range(views):
-        count = count + weight[v : v + 1, :]
-        seen = seen + weight[v : v + 1, :] * jnp.sum(obs[v].reshape(-1, 8, lanes), axis=0)
-    stat[0:1] = jnp.sum(seen / count, axis=0, keepdims=True)
-
-    arrive(out_copies)
+        weight_v = weight_of(mine, v)
+        count = count + weight_v
+        seen = seen + weight_v * jnp.sum(obs[v].reshape(-1, 8, lanes), axis=0)
+    count = count[0:1]
+    stat[0:1] = jnp.sum(seen, axis=0, keepdims=True) / count
+    for hop in range(5, rounds):
+        meet(hop)
+
+    arrive(out_copies((1, 2, 3)))
     lane = lax.broadcasted_iota(jnp.int32, (wide_y, lanes), 1)
     high, low = split(ext[...].reshape(wide_x * wide_y, lanes))
     ext_hi[:, :lanes] = high
     ext_lo[:, :lanes] = low
     for g in range(groups):
         merged = jnp.where(lane % (2 * rad) < rad, from_left[g], from_right[g])
+        edge[g] = merged
         for i in range(8):
             shift = (lanes - 2 * rad * i) % lanes
             rolled = pltpu.roll(merged, shift, 1) if shift else merged
@@ -292,19 +347,25 @@
             ext_lo[first : first + wide_y, lanes:] = low
 
     thin = lax.broadcasted_iota(jnp.int32, (rad, lanes), 1)
+    everyone = jnp.concatenate([weight[slot] for slot in range(27)] + [jnp.zeros((5, lanes), F32)], axis=0)
+    counts = jnp.zeros(everyone.shape, F32)
     for v in range(views):
+        theirs = weight_of(everyone, v)
+        counts = counts + theirs
+
+        def spread_of(dx, dy, dz):
+            slot = 9 * dz + 3 * dx + dy
+            return jnp.broadcast_to(theirs[slot : slot + 1], (rad, lanes))
+
         for dx in range(3):
             for dy in range(3):
-                mid = jnp.broadcast_to(weight_xy[dx, dy, v : v + 1, :], (rad, lanes))
-                left = jnp.broadcast_to(weight_left[dx, dy, v : v + 1, :], (rad, lanes))
-                right = jnp.broadcast_to(weight_right[dx, dy, v : v + 1, :], (rad, lanes))
+                mid, left, right = (spread_of(dx, dy, dz) for dz in (1, 0, 2))
                 side = jnp.where(thin < rad, left, jnp.where(thin < 2 * rad, right, 0.0))
-                for first in range(0 if dy == 0 else (rad if dy == 1 else rad + cols), rad if dy == 0 else (rad + cols if dy == 1 else wide_y), rad):
-                    scale[v, dx, first : first + rad, :lanes] = mid
-                    scale[v, dx, first : first + rad, lanes:] = side
-
-    total[...] = jnp.zeros(total.shape, F32)
-    fringe[...] = jnp.zeros(fringe.shape, F32)
+                first, last = ((0, rad), (rad, rad + cols), (rad + cols, wide_y))[dy]
+                for at in range(first, last, rad):
+                    scale[v, dx, at : at + rad, :lanes] = mid
+                    scale[v, dx, at : at + rad, lanes:] = side
+    inverses[...] = jnp.where(counts > 0.0, 1.0 / jnp.maximum(counts, 1.0), 0.0)
 
     def one_view(v, carry):
         size = 8 * wide_y
@@ -349,8 +410,49 @@
         for i in range(1, 8):
             merged = merged + pltpu.roll(fringe[8 * g + i], 2 * rad * i, 1)
         back_pack[g] = merged
-    start(back_copies)
-    arrive(back_copies)
+    seen = jnp.zeros((8, lanes), F32)
+    for dx in range(3):
+        for dy in range(3):
+            first_y, last_y = ((0, rad), (rad, rad + cols), (rad + cols, wide_y))[dy]
+            first_x, last_x = ((0, rad), (rad, rad + rows), (rad + rows, wide_x))[dx]
+            part_y = slice(first_y, last_y)
+            part = total[first_x:last_x, part_y, :] * ext[first_x:last_x, part_y, :]
+            part = jnp.sum(part.reshape(-1, 8, lanes), axis=0)
+            slot = 9 + 3 * dx + dy
+            seen = seen + part * inverses[slot : slot + 1, :]
+            part_x = slice(first_x // 8, last_x // 8)
+            part = back_pack[part_x, part_y, :] * edge[part_x, part_y, :]
+            part = jnp.sum(part.reshape(-1, 8, lanes), axis=0)
+            left, right = (inverses[at : at + 1, :] for at in (slot - 9, slot + 9))
+            seen = seen + part * jnp.where(lane[0:1] % (2 * rad) < rad, left, right)
+    stat[1:2] = jnp.sum(seen, axis=0, keepdims=True)
+
+    def sums_a():
+        for slot, offset in enumerate(ring_a):
+            yield pltpu.make_async_remote_copy(
+                src_ref=stat,
+                dst_ref=stat_a.at[slot],
+                send_sem=a_send.at[slot],
+                recv_sem=a_recv.at[slot],
+                device_id=partner(*offset),
+                device_id_type=MESH,
+            )
+
+    def sums_b():
+        for slot, offset in enumerate(ring_b):
+            yield pltpu.make_async_remote_copy(
+                src_ref=part_a,
+                dst_ref=stat_b.at[slot],
+                send_sem=b_send.at[slot],
+                recv_sem=b_recv.at[slot],
+                device_id=partner(*offset),
+                device_id_type=MESH,
+            )
+
+    for copy in sums_a():
+        copy.start()
+    start(back_copies())
+    arrive(back_copies())
     near = back_xy[...]
 
     def fold(values, size, rad, axis):
@@ -369,39 +471,12 @@
     ends = fold(fold(ends, pack_rows, pack_rad, 0), cols, rad, 1)
     lane = lax.broadcasted_iota(jnp.int32, (cols, lanes), 1)
     outer = (lane < rad) | (lane >= lanes - rad)
-    seen = jnp.zeros((8, lanes), F32)
     for x in range(rows):
         rolled = pltpu.roll(ends[x // 8], lanes - (2 * rad * (x % 8) + rad), 1)
         summed = total[rad + x, rad : rad + cols, :] + near[x] + jnp.where(outer, rolled, 0.0)
-        updated = est_ref[x] * (summed / count)
+        updated = ext[rad + x, own_y, :] * (summed / count)
         out_ref[x] = updated
-        seen = seen + jnp.sum(updated.reshape(-1, 8, lanes), axis=0)
-    stat[1:2] = jnp.sum(seen, axis=0, keepdims=True)
-
-    def sums_a():
-        for slot, offset in enumerate(ring_a):
-            yield pltpu.make_async_remote_copy(
-                src_ref=stat,
-                dst_ref=stat_a.at[slot],
-                send_sem=a_send.at[slot],
-                recv_sem=a_recv.at[slot],
-                device_id=partner(*offset),
-                device_id_type=MESH,
-            )
-
-    def sums_b():
-        for slot, offset in enumerate(ring_b):
-            yield pltpu.make_async_remote_copy(
-                src_ref=part_a,
-                dst_ref=stat_b.at[slot],
-                send_sem=b_send.at[slot],
-                recv_sem=b_recv.at[slot],
-                device_id=partner(*offset),
-                device_id_type=MESH,
-            )
-
-    for copy in sums_a():
-        copy.start()
+
     for copy in sums_a():
         copy.wait_recv()
     everything = stat[...] + jnp.sum(stat_a[...], axis=0)
@@ -417,7 +492,7 @@
     factor = jnp.broadcast_to(wanted, (1, lanes)) / jnp.broadcast_to(gotten, (1, lanes))
     out_ref[...] = out_ref[...] * factor.reshape(1, 1, lanes)
 
-    for family in (out_copies, back_copies):
+    for family in (out_copies((1, 2, 3)), back_copies()):
         leave(family)
     for copy in sums_a():
         copy.wait_send()
@@ -440,7 +515,10 @@
     def dma(*shape):
         return pltpu.SemaphoreType.DMA(shape)
 
+    views_all, dims, length = psf_taps.shape
     scratch = [
+        pltpu.SMEM((dims, views_all, length), F32),
+        pltpu.SMEM((views,), jnp.int32),
         vm(*observed.shape),
         vm(wide_x, wide_y, lanes),
         vm(wide_x * wide_y, 2 * lanes, dtype=BF16),
@@ -448,11 +526,10 @@
         vm(rows // 8, cols, lanes),
         vm(groups, wide_y, lanes),
         vm(groups, wide_y, lanes),
-        vm(views, lanes),
-        vm(3, 3, views, lanes),
-        vm(3, 3, views, lanes),
-        vm(3, 3, views, lanes),
+        vm(groups, wide_y, lanes),
+        vm(27, 1, lanes),
         vm(views, 3, wide_y, 2 * lanes),
+        vm(32, lanes),
         vm(views, 2 * lanes, 2 * lanes, dtype=BF16),
         vm(views, 2 * lanes, 2 * lanes, dtype=BF16),
         vm(views, 8 * cols, 8 * wide_y, dtype=BF16),
@@ -470,11 +547,12 @@
         vm(n_a, 2, lanes),
         vm(n_b, 2, lanes),
         vm(2, lanes),
-        pltpu.SemaphoreType.DMA,
-        dma(26, 2),
-        dma(26, 2),
-        dma(26),
-        dma(26),
+        dma(4),
+        pltpu.SemaphoreType.REGULAR((max(1, sum(sizes) - 4),)),
+        dma(27, 2),
+        dma(27, 2),
+        dma(27),
+        dma(27),
         dma(n_a),
         dma(n_a),
         dma(n_b),
@@ -484,9 +562,9 @@
         functools.partial(kernel, sizes),
         out_shape=jax.ShapeDtypeStruct(estimate.shape, F32),
         in_specs=[
-            pl.BlockSpec(memory_space=pltpu.SMEM),
-            pl.BlockSpec(memory_space=pltpu.SMEM),
-            pl.BlockSpec(memory_space=pltpu.VMEM),
+            pl.BlockSpec(memory_space=pl.ANY),
+            pl.BlockSpec(memory_space=pl.ANY),
+            pl.BlockSpec(memory_space=pl.ANY),
             pl.BlockSpec(memory_space=pl.ANY),
         ],
         out_specs=pl.BlockSpec(memory_space=pltpu.VMEM),

time: 41.1 us -> 36.2 us (0.88)
  Pallas kernels: 39.3 us -> 34.4 us
    pallas_call x1, Pallas kernels: 39.3 us -> 34.4 us  [on_device(): pl.pallas_call(functools.partial(kernel, sizes), out_shape=jax.ShapeDtype...]
where the time goes in v1:
time: 36.2 us; the launch traced here: 36 us
  Pallas kernels  34.4 us (95%)
  local copies, waits for them, and re-layouts  1.57 us (4%)
    pallas_call x1, Pallas kernels, on_device(): pl.pallas_call(functools.partial(kernel, sizes), out_shape=jax.ShapeDtype...  34.4 us
    unnamed x1, local copies, waits for them, and re-layouts  1.57 us

profile of v1, /device:TPU:0, one launch (start us, length us, event | category | flops | bytes accessed | tf_op | source)
XLA Modules:
  0.0 36.0 jit_solution(3658277490120407901)
XLA Ops:
  0.0 34.4 %shard_map.46 = f32[16,16,128]{2,1,0:T(8,128)} custom-call(f32[3,8,17]{2,1,0:T(8,128)} %bitcast.2, s32[8]{0:T(128)} %bitcast.3, f32[16,16,128]{2,1,0:T(8,128)} %est_hbm.1, f32[8,16,16,128]{3,2,1,0:T(8,128)} %obs_hbm.1), custom_call_target="tpu_custom_call" | custom-call | tf_op jit(solution)/shard_map/pallas_call | solution.py:561
  34.5 1.6 %copy.6 = f32[16,16,128]{2,1,0:T(8,128)} copy(f32[16,16,128]{2,1,0:T(8,128)} %shard_map.46) | data formatting | bytes 262144

commit v2 on v1

--- a/solution.py
+++ b/solution.py
@@ -46,6 +46,7 @@
     est_hbm,
     obs_hbm,
     out_ref,
+    factor_ref,
     taps_ref,
     cover_ref,
     obs,
@@ -76,6 +77,7 @@
     stat_a,
     stat_b,
     part_a,
+    marks,
     fetch_sem,
     hop_sem,
     out_send,
@@ -210,54 +212,68 @@
                 pltpu.make_async_remote_copy(
                     src_ref=pair[0],
                     dst_ref=pair[1],
-                    send_sem=out_send.at[slot, which],
-                    recv_sem=out_recv.at[slot, which],
+                    send_sem=out_send,
+                    recv_sem=out_recv,
                     device_id=device(dx, dy, dz),
                     device_id_type=MESH,
                 )
                 for which, pair in enumerate(pairs)
             ]
-            yield exists(dx, dy, dz), exists(-dx, -dy, -dz), copies
+            yield exists(dx, dy, dz), copies
 
     def back_copies():
         for dx, dy, dz in sorted(around, key=lambda offset: abs(offset[2])):
-            slot = slot_of(dx, dy, dz)
             size, width = (rows, rad) if dz == 0 else (pack_rows, pack_rad)
             source = total if dz == 0 else back_pack
             target = (back_right, back_xy, back_left)[dz + 1]
             copy = pltpu.make_async_remote_copy(
                 src_ref=source.at[wide(dx, size, width), wide(dy, cols, rad), :],
                 dst_ref=target.at[wide(-dx, size, width), wide(-dy, cols, rad), :],
-                send_sem=back_send.at[slot],
-                recv_sem=back_recv.at[slot],
+                send_sem=back_send,
+                recv_sem=back_recv,
                 device_id=device(dx, dy, dz),
                 device_id_type=MESH,
             )
-            yield exists(dx, dy, dz), exists(-dx, -dy, -dz), [copy]
+            yield exists(dx, dy, dz), [copy]
 
     def start(family):
-        for sends, _, copies in family:
+        for sends, copies in family:
 
             @pl.when(sends)
             def _():
                 for copy in copies:
                     copy.start()
 
-    def arrive(family):
-        for _, takes, copies in family:
-
-            @pl.when(takes)
-            def _():
-                for copy in copies:
-                    copy.wait_recv()
-
-    def leave(family):
-        for sends, _, copies in family:
-
-            @pl.when(sends)
-            def _():
-                for copy in copies:
-                    copy.wait_send()
+    def drain(semaphore, amount):
+        bytes_of = marks.at[pl.ds(0, amount)]
+        pltpu.make_async_remote_copy(
+            src_ref=bytes_of,
+            dst_ref=bytes_of,
+            send_sem=semaphore,
+            recv_sem=semaphore,
+            device_id=partner(*ring_all[0]),
+            device_id_type=MESH,
+        ).wait_recv()
+
+    def drain_all(semaphore, extra):
+        counts_of = [
+            (min(count - 1, 2), (me > 0).astype(jnp.int32) + (me < count - 1).astype(jnp.int32))
+            for me, count in ((me_x, n_x), (me_y, n_y), (me_z, n_z))
+        ]
+        for c_x in range(min(1, n_x - 1), counts_of[0][0] + 1):
+            for c_y in range(min(1, n_y - 1), counts_of[1][0] + 1):
+                for c_z in range(min(1, n_z - 1), counts_of[2][0] + 1):
+                    amount = 0
+                    for dx, dy, dz in ((i, j, k) for i in (0, 1) for j in (0, 1) for k in (0, 1)):
+                        if (dx, dy, dz) == (0, 0, 0):
+                            continue
+                        size, width = (rows, rad) if dz == 0 else (pack_rows, pack_rad)
+                        message = (width if dx else size) * (rad if dy else cols) + extra
+                        amount += (c_x if dx else 1) * (c_y if dy else 1) * (c_z if dz else 1) * message
+
+                    @pl.when((counts_of[0][1] == c_x) & (counts_of[1][1] == c_y) & (counts_of[2][1] == c_z))
+                    def _():
+                        drain(semaphore, amount)
 
     def build(v, carry):
         def summed(dim):
@@ -305,10 +321,10 @@
     meet(0)
     start(out_copies((1,)))
     loads[2].wait()
-    stops = [min(stop, views) for stop in (0, 2, 4, 6, views)]
-    for hop in range(1, 5):
+    stops = [min(stop, views) for stop in (0, 2, 4, views)]
+    for hop in range(1, 4):
         lax.fori_loop(stops[hop - 1], stops[hop], build, 0)
-        if hop < rounds:
+        if hop < min(3, rounds):
             meet(hop)
         if hop in (1, 2):
             start(out_copies((hop + 1,)))
@@ -327,10 +343,8 @@
         seen = seen + weight_v * jnp.sum(obs[v].reshape(-1, 8, lanes), axis=0)
     count = count[0:1]
     stat[0:1] = jnp.sum(seen, axis=0, keepdims=True) / count
-    for hop in range(5, rounds):
-        meet(hop)
-
-    arrive(out_copies((1, 2, 3)))
+
+    drain_all(out_recv, 1)
     lane = lax.broadcasted_iota(jnp.int32, (wide_y, lanes), 1)
     high, low = split(ext[...].reshape(wide_x * wide_y, lanes))
     ext_hi[:, :lanes] = high
@@ -403,7 +417,20 @@
             fringe[8 * g : 8 * g + 8] += piece[:, :, lanes:]
         return carry
 
-    lax.fori_loop(0, views, one_view, 0, unroll=2)
+    width_of = 2 if views % 2 == 0 else 1
+
+    def some_views(p, carry):
+        for hop in range(3, rounds):
+
+            @pl.when(p == min(hop - 3, views // width_of - 1))
+            def _():
+                meet(hop)
+
+        for v in range(width_of):
+            one_view(width_of * p + v, carry)
+        return carry
+
+    lax.fori_loop(0, views // width_of, some_views, 0)
 
     for g in range(groups):
         merged = fringe[8 * g]
@@ -432,8 +459,8 @@
             yield pltpu.make_async_remote_copy(
                 src_ref=stat,
                 dst_ref=stat_a.at[slot],
-                send_sem=a_send.at[slot],
-                recv_sem=a_recv.at[slot],
+                send_sem=a_send,
+                recv_sem=a_recv,
                 device_id=partner(*offset),
                 device_id_type=MESH,
             )
@@ -443,8 +470,8 @@
             yield pltpu.make_async_remote_copy(
                 src_ref=part_a,
                 dst_ref=stat_b.at[slot],
-                send_sem=b_send.at[slot],
-                recv_sem=b_recv.at[slot],
+                send_sem=b_send,
+                recv_sem=b_recv,
                 device_id=partner(*offset),
                 device_id_type=MESH,
             )
@@ -452,7 +479,7 @@
     for copy in sums_a():
         copy.start()
     start(back_copies())
-    arrive(back_copies())
+    drain_all(back_recv, 0)
     near = back_xy[...]
 
     def fold(values, size, rad, axis):
@@ -477,27 +504,24 @@
         updated = ext[rad + x, own_y, :] * (summed / count)
         out_ref[x] = updated
 
-    for copy in sums_a():
-        copy.wait_recv()
+    drain(a_recv, 2 * len(ring_a))
     everything = stat[...] + jnp.sum(stat_a[...], axis=0)
     if ring_b:
         part_a[...] = everything
         for copy in sums_b():
             copy.start()
-        for copy in sums_b():
-            copy.wait_recv()
+        drain(b_recv, 2 * len(ring_b))
         everything = part_a[...] + jnp.sum(stat_b[...], axis=0)
     wanted = jnp.sum(everything[0:1], axis=1, keepdims=True)
     gotten = jnp.sum(everything[1:2], axis=1, keepdims=True)
     factor = jnp.broadcast_to(wanted, (1, lanes)) / jnp.broadcast_to(gotten, (1, lanes))
-    out_ref[...] = out_ref[...] * factor.reshape(1, 1, lanes)
-
-    for family in (out_copies((1, 2, 3)), back_copies()):
-        leave(family)
-    for copy in sums_a():
-        copy.wait_send()
-    for copy in sums_b():
-        copy.wait_send()
+    factor_ref[...] = factor
+
+    drain_all(out_send, 1)
+    drain_all(back_send, 0)
+    drain(a_send, 2 * len(ring_a))
+    if ring_b:
+        drain(b_send, 2 * len(ring_b))
 
 
 def on_device(sizes, estimate, observed, coverage, psf_taps):
@@ -514,6 +538,9 @@
 
     def dma(*shape):
         return pltpu.SemaphoreType.DMA(shape)
+
+    def in_hbm(values):
+        return pltpu.with_memory_space_constraint(values, pltpu.HBM)
 
     views_all, dims, length = psf_taps.shape
     scratch = [
@@ -547,30 +574,25 @@
         vm(n_a, 2, lanes),
         vm(n_b, 2, lanes),
         vm(2, lanes),
+        vm(5 * rows * cols, 1, lanes),
         dma(4),
         pltpu.SemaphoreType.REGULAR((max(1, sum(sizes) - 4),)),
-        dma(27, 2),
-        dma(27, 2),
-        dma(27),
-        dma(27),
-        dma(n_a),
-        dma(n_a),
-        dma(n_b),
-        dma(n_b),
+        *[pltpu.SemaphoreType.DMA] * 8,
     ]
-    return pl.pallas_call(
+    updated, factor = pl.pallas_call(
         functools.partial(kernel, sizes),
-        out_shape=jax.ShapeDtypeStruct(estimate.shape, F32),
+        out_shape=(jax.ShapeDtypeStruct(estimate.shape, F32), jax.ShapeDtypeStruct((1, lanes), F32)),
         in_specs=[
             pl.BlockSpec(memory_space=pl.ANY),
             pl.BlockSpec(memory_space=pl.ANY),
             pl.BlockSpec(memory_space=pl.ANY),
             pl.BlockSpec(memory_space=pl.ANY),
         ],
-        out_specs=pl.BlockSpec(memory_space=pltpu.VMEM),
+        out_specs=(pl.BlockSpec(memory_space=pltpu.VMEM), pl.BlockSpec(memory_space=pltpu.VMEM)),
         scratch_shapes=scratch,
-        compiler_params=pltpu.CompilerParams(collective_id=0, has_side_effects=True),
-    )(jnp.transpose(psf_taps, (1, 0, 2)), coverage.reshape(views), estimate, observed)
+        compiler_params=pltpu.CompilerParams(collective_id=0, has_side_effects=True, vmem_limit_bytes=40 * 1024 * 1024),
+    )(*map(in_hbm, (jnp.transpose(psf_taps, (1, 0, 2)), coverage.reshape(views), estimate, observed)))
+    return updated * factor.reshape(1, 1, lanes)
 
 
 def solution(mesh):

time: 36.2 us -> 31.5 us (0.87)
  Pallas kernels: 34.4 us -> 30.6 us
  local copies, waits for them, and re-layouts: 1.57 us -> 0 us
  other arithmetic: 0 us -> 0.67 us
    pallas_call x1, Pallas kernels: 34.4 us -> 30.6 us  [on_device(): pl.pallas_call(functools.partial(kernel, sizes), out_shape=(jax.ShapeDtyp...]
    unnamed x1 -> x0, local copies, waits for them, and re-layouts: 1.57 us -> none
    mul x0 -> x1, other arithmetic: none -> 0.67 us  [on_device(): return updated * factor.reshape(1, 1, lanes)]
where the time goes in v2:
time: 31.5 us; the launch traced here: 31.3 us
  Pallas kernels  30.6 us (97%)
  other arithmetic  0.67 us (2%)
    pallas_call x1, Pallas kernels, on_device(): pl.pallas_call(functools.partial(kernel, sizes), out_shape=(jax.ShapeDtyp...  30.6 us
    mul x1, other arithmetic, on_device(): return updated * factor.reshape(1, 1, lanes)  0.67 us

profile of v2, /device:TPU:0, one launch (start us, length us, event | category | flops | bytes accessed | tf_op | source)
XLA Modules:
  0.0 31.3 jit_solution(2245636537551741509)
XLA Ops:
  0.0 30.6 %shard_map.46 = (f32[16,16,128]{2,1,0:T(8,128)S(1)}, f32[1,128]{1,0:T(1,128)S(1)}) custom-call(f32[3,8,17]{2,1,0:T(8,128)} %bitcast.4, s32[8]{0:T(128)} %bitcast.5, f32[16,16,128]{2,1,0:T(8,128)} %est_hbm.1, f32[8,16,16,128]{3,2,1,0:T(8,128)} %obs_hbm.1), custom_call_target="tpu_custom_call" | custom-call | tf_op jit(solution)/shard_map/pallas_call | solution.py:582
  30.6 0.7 %broadcast_multiply_fusion = f32[16,16,128]{2,1,0:T(8,128)} fusion(f32[16,16,128]{2,1,0:T(8,128)S(1)} %get-tuple-element.7, f32[128]{0:T(128)S(1)} %bitcast.3), kind=kLoop, calls=%fused_computation | loop fusion | flops 32768 | bytes 262656 | tf_op jit(solution)/shard_map/mul | solution.py:595

commit v3 on v2

--- a/solution.py
+++ b/solution.py
@@ -51,24 +51,29 @@
     cover_ref,
     obs,
     ext,
-    ext_hi,
-    ext_lo,
+    wide_a,
+    wide_b,
     pack,
     from_left,
     from_right,
     edge,
     weight,
-    scale,
     inverses,
-    band,
-    twin,
-    gath_hi,
-    gath_lo,
+    mask,
+    mask_edge,
+    ahead_a,
+    ahead_b,
+    gath,
     scat,
+    astern,
+    astern_edge,
+    taps_x,
+    scat_edge,
+    blurred,
     lined,
     spread,
+    fringe,
     total,
-    fringe,
     back_pack,
     back_left,
     back_right,
@@ -275,59 +280,96 @@
                     def _():
                         drain(semaphore, amount)
 
-    def build(v, carry):
-        def summed(dim):
-            values = [taps_ref[dim, v, k] for k in range(length)]
-            while len(values) > 1:
-                values = [sum(values[i : i + 2]) for i in range(0, len(values), 2)]
-            return jnp.full((8, lanes), values[0], F32)
-
-        inverse = 1.0 / (summed(0) * summed(1) * summed(2))
-
-        def chosen(offset, dim):
-            result = jnp.zeros(offset.shape, F32)
-            for k in range(length):
-                result = jnp.where(offset == k, taps_ref[dim, v, k], result)
-            return result
-
-        def iota(shape, dim):
-            return lax.broadcasted_iota(jnp.int32, shape, dim)
-
-        shape = (lanes, lanes)
-        main = chosen(iota(shape, 0) - iota(shape, 1) + rad, 2)
-        shape = (2 * rad, lanes)
-        row, col = iota(shape, 0), iota(shape, 1)
-        edge = chosen(jnp.where(row < rad, row, row + lanes) - col, 2)
-        for first, part in ((0, main), (lanes, edge)):
-            part = (part.reshape(-1, 8, lanes) * inverse[None]).reshape(part.shape)
-            high, low = split(part)
-            band[v, first : first + part.shape[0], :] = jnp.concatenate([high, low], axis=1)
-            twin[v, first : first + part.shape[0], :] = jnp.concatenate([high, high], axis=1)
-        rest = band.shape[1] - lanes - 2 * rad
-        band[v, lanes + 2 * rad :, :] = jnp.zeros((rest, 2 * lanes), BF16)
-        twin[v, lanes + 2 * rad :, :] = jnp.zeros((rest, 2 * lanes), BF16)
-        shape = (8 * cols, 8 * wide_y)
-        row, col = iota(shape, 0), iota(shape, 1)
-        offset = jnp.where(row // cols == col // wide_y, col % wide_y - row % cols, -1)
-        high, low = split(chosen(offset, 1))
-        gath_hi[v], gath_lo[v] = high, low
-        shape = (8 * wide_y, 8 * cols)
-        row, col = iota(shape, 0), iota(shape, 1)
-        offset = jnp.where(row // wide_y == col // cols, row % wide_y - col % cols, -1)
-        high, low = split(chosen(offset, 1))
-        scat[v] = jnp.concatenate([high, low], axis=1)
+    def iota(shape, dim):
+        return lax.broadcasted_iota(jnp.int32, shape, dim)
+
+    span = 2 * rad
+    block = lanes // wide_y
+
+    def stack(*parts):
+        return jnp.concatenate(parts, axis=0)
+
+    def beside(*parts):
+        return jnp.concatenate(parts, axis=1)
+
+    def build(p, carry):
+        for j in range(2):
+            v = 2 * p + j
+
+            def summed(dim):
+                values = [taps_ref[dim, v, k] for k in range(length)]
+                while len(values) > 1:
+                    values = [sum(values[i : i + 2]) for i in range(0, len(values), 2)]
+                return jnp.full((8, lanes), values[0], F32)
+
+            inverse = 1.0 / (summed(0) * summed(1) * summed(2))
+
+            def chosen(offset, dim):
+                result = jnp.zeros(offset.shape, F32)
+                for k in range(length):
+                    result = jnp.where(offset == k, taps_ref[dim, v, k], result)
+                return result
+
+            def scaled(part):
+                return (part.reshape(-1, 8, lanes) * inverse[None]).reshape(part.shape)
+
+            here = slice(j * lanes, (j + 1) * lanes)
+            square = (lanes, lanes)
+            main = scaled(chosen(iota(square, 0) - iota(square, 1) + rad, 2))
+            row, col = iota((span, lanes), 0), iota((span, lanes), 1)
+            edges = scaled(chosen(jnp.where(row < rad, row, row + lanes) - col, 2))
+            high, low = split(main)
+            ahead_a[p, :, here] = stack(high, high)
+            ahead_b[p, :lanes, here] = low
+            high, low = split(edges)
+            ahead_b[p, lanes:, here] = stack(high, high, low, jnp.zeros((lanes - 3 * span, lanes), BF16))
+            high, low = split(main.T)
+            astern[v] = stack(beside(high, low), beside(high, jnp.zeros(square, BF16)))
+            turned = jnp.where(iota(square, 1) // span == v, stack(*[edges] * views).T, 0.0)
+            high, low = split(turned)
+            astern_edge[v] = stack(beside(high, low), beside(high, jnp.zeros(square, BF16)))
+            shape = (block * cols, lanes)
+            row, col = iota(shape, 0), iota(shape, 1)
+            offset = jnp.where(row // cols == col // wide_y, col % wide_y - row % cols, -1)
+            blur_y = chosen(offset, 1)
+            high, low = split(blur_y)
+            gath[v] = stack(beside(high, high), beside(low, jnp.zeros(shape, BF16)))
+            turned = blur_y.T
+            high = turned.astype(BF16).astype(F32)
+            low = turned - high
+            scat[v] = beside(high, high, low).astype(BF16)
         return carry
+
+    def lines_of(dim):
+        lane = iota((1, lanes), 1)
+        lines = []
+        for k in range(length):
+            line = jnp.zeros((1, lanes), F32)
+            for v in range(views):
+                line = jnp.where(lane // span == v, taps_ref[dim, v, k], line)
+            lines.append(line)
+        return lines
 
     meet(0)
     start(out_copies((1,)))
     loads[2].wait()
-    stops = [min(stop, views) for stop in (0, 2, 4, views)]
+    stops = [min(stop, views // 2) for stop in (0, 1, 2, views // 2)]
     for hop in range(1, 4):
         lax.fori_loop(stops[hop - 1], stops[hop], build, 0)
         if hop < min(3, rounds):
             meet(hop)
         if hop in (1, 2):
             start(out_copies((hop + 1,)))
+
+    for k, line in enumerate(lines_of(0)):
+        taps_x[k : k + 1] = line
+    shape = (wide_y, lanes)
+    offset = iota(shape, 0) - iota(shape, 1) % cols
+    base = jnp.zeros(shape, F32)
+    for k, line in enumerate(lines_of(1)):
+        base = jnp.where(offset == k, line, base)
+    high = base.astype(BF16).astype(F32)
+    scat_edge[...] = beside(high, high, base - high)
 
     loads[3].wait()
     def weight_of(rows_of, v):
@@ -345,98 +387,134 @@
     stat[0:1] = jnp.sum(seen, axis=0, keepdims=True) / count
 
     drain_all(out_recv, 1)
-    lane = lax.broadcasted_iota(jnp.int32, (wide_y, lanes), 1)
     high, low = split(ext[...].reshape(wide_x * wide_y, lanes))
-    ext_hi[:, :lanes] = high
-    ext_lo[:, :lanes] = low
+    wide_a[:, :lanes] = high
+    wide_a[:, lanes:] = low
+    wide_b[:, :lanes] = high
+    lane = iota((wide_y, lanes), 1)
     for g in range(groups):
-        merged = jnp.where(lane % (2 * rad) < rad, from_left[g], from_right[g])
+        merged = jnp.where(lane % span < rad, from_left[g], from_right[g])
         edge[g] = merged
+        high = merged.astype(BF16).astype(F32)
+        low = merged - high
+        count_of = lanes // span
+        highs = [pltpu.roll(high, span * i, 1) if i else high for i in range(count_of)]
+        lows = [pltpu.roll(low, span * i, 1) if i else low for i in range(count_of)]
         for i in range(8):
-            shift = (lanes - 2 * rad * i) % lanes
-            rolled = pltpu.roll(merged, shift, 1) if shift else merged
-            high, low = split(rolled)
+            third = jnp.where(lane < 2 * span, lows[(1 - i) % count_of], highs[(2 - i) % count_of])
+            terms = jnp.where(lane < span, highs[-i % count_of], third)
             first = (8 * g + i) * wide_y
-            ext_hi[first : first + wide_y, lanes:] = high
-            ext_lo[first : first + wide_y, lanes:] = low
-
-    thin = lax.broadcasted_iota(jnp.int32, (rad, lanes), 1)
-    everyone = jnp.concatenate([weight[slot] for slot in range(27)] + [jnp.zeros((5, lanes), F32)], axis=0)
+            wide_b[first : first + wide_y, lanes:] = terms.astype(BF16)
+
+    everyone = stack(*[weight[slot] for slot in range(27)], jnp.zeros((5, lanes), F32))
     counts = jnp.zeros(everyone.shape, F32)
+
+    def along_y(rows_of, first):
+        bands = [(rad, 0), (cols, 1), (rad, 2)]
+        return stack(*[jnp.broadcast_to(rows_of[first + dy : first + dy + 1], (size, lanes)) for size, dy in bands])
+
     for v in range(views):
         theirs = weight_of(everyone, v)
         counts = counts + theirs
-
-        def spread_of(dx, dy, dz):
-            slot = 9 * dz + 3 * dx + dy
-            return jnp.broadcast_to(theirs[slot : slot + 1], (rad, lanes))
-
         for dx in range(3):
-            for dy in range(3):
-                mid, left, right = (spread_of(dx, dy, dz) for dz in (1, 0, 2))
-                side = jnp.where(thin < rad, left, jnp.where(thin < 2 * rad, right, 0.0))
-                first, last = ((0, rad), (rad, rad + cols), (rad + cols, wide_y))[dy]
-                for at in range(first, last, rad):
-                    scale[v, dx, at : at + rad, :lanes] = mid
-                    scale[v, dx, at : at + rad, lanes:] = side
+            mask[v, dx] = along_y(theirs, 9 + 3 * dx).astype(BF16)
+    for dx in range(3):
+        for side in range(2):
+            part = along_y(everyone, 18 * side + 3 * dx)
+            terms = scat_edge[...] * beside(part, part, part)
+            mask_edge[dx, side * wide_y : (side + 1) * wide_y] = terms.astype(BF16)
     inverses[...] = jnp.where(counts > 0.0, 1.0 / jnp.maximum(counts, 1.0), 0.0)
 
-    def one_view(v, carry):
+    def side_of(g):
+        return 0 if 8 * g < rad else (1 if 8 * g < rad + rows else 2)
+
+    def spread_x(source, tap):
+        pieces = []
+        for e in range(wide_x):
+            piece = None
+            for a in range(rows):
+                if 0 <= e - a < length:
+                    term = tap(e - a) * source[a]
+                    piece = term if piece is None else piece + term
+            pieces.append(piece)
+        return pieces
+
+    def pairs_of(part, half):
+        return beside(part[:half], part[half:])
+
+    def two_views(p):
+        blurred[...] = dot(wide_a[...], ahead_a[p]) + dot(wide_b[...], ahead_b[p])
         size = 8 * wide_y
-        high_part = slice(0, lanes)
+        scattered = []
+        for j in range(2):
+            v = 2 * p + j
+            for g in range(groups):
+                high, low = split(blurred[g * size : (g + 1) * size, j * lanes : (j + 1) * lanes])
+                line = dot(gath[v], stack(pairs_of(high, size // 2), pairs_of(low, size // 2)))
+                half = block * cols
+                line = line[:half] + line[half:]
+                for which in range(2):
+                    first = 8 * g + which * block
+                    lined[j, first : first + block] = line[:, which * lanes : (which + 1) * lanes].reshape(block, cols, lanes)
+            blur = taps_ref[0, v, 0] * lined[j, 0:rows]
+            for k in range(1, length):
+                blur = blur + taps_ref[0, v, k] * lined[j, k : k + rows]
+            ratio = (obs[v] / blur).reshape(rows * cols, lanes)
+            ratio = beside(*split(ratio))
+            back = folded(dot(ratio, astern[v]))
+            fringe[...] += dot(ratio, astern_edge[v])
+            spread[j] = back.reshape(rows, cols, lanes)
+            pieces = spread_x(spread.at[j], lambda k: taps_ref[0, v, k])
+            sent = []
+            for g in range(groups):
+                high, low = split(stack(*pieces[8 * g : 8 * g + 8]))
+                high, low = (pairs_of(part, block * cols) for part in (high, low))
+                sent.append(stack(high, low, high))
+            scattered.append(sent)
         for g in range(groups):
-            here = slice(g * size, (g + 1) * size)
-            blurred = folded(dot(ext_hi[here, :], band[v])) + dot(ext_lo[here, :], band[v, :, high_part])
-            high, low = split(blurred)
-            line = folded(dot(gath_hi[v], jnp.concatenate([high, low], axis=1))) + dot(gath_lo[v], high)
-            lined[8 * g : 8 * g + 8] = line.reshape(8, cols, lanes)
-        blur = taps_ref[0, v, 0] * lined[0:rows]
-        for k in range(1, length):
-            blur = blur + taps_ref[0, v, k] * lined[k : k + rows]
-        spread[...] = obs[v] / blur
-        for g in range(groups):
-            pieces = []
-            for e in range(8 * g, 8 * g + 8):
-                piece = None
-                for a in range(rows):
-                    if 0 <= e - a < length:
-                        term = taps_ref[0, v, e - a] * spread[a]
-                        piece = term if piece is None else piece + term
-                pieces.append(piece)
-            piece = jnp.concatenate(pieces, axis=0)
-            both = jnp.concatenate(split(piece), axis=1)
-            piece = folded(dot(scat[v], jnp.concatenate([both, both], axis=0)))
-            high, low = split(piece)
-            flip = ((1,), (1,))
-            piece = dot(jnp.concatenate([high, low], axis=1), twin[v], flip)
-            piece = piece + dot(high, band[v, :, lanes:], flip)
-            piece = piece.reshape(8, wide_y, 2 * lanes)
-            dx = 0 if 8 * g < rad else (1 if 8 * g < rad + rows else 2)
-            piece = piece * scale[v, dx][None]
-            total[8 * g : 8 * g + 8] += piece[:, :, :lanes]
-            fringe[8 * g : 8 * g + 8] += piece[:, :, lanes:]
-        return carry
-
-    width_of = 2 if views % 2 == 0 else 1
+            dx = side_of(g)
+            reach = None
+            for j in range(2):
+                v = 2 * p + j
+                here = stack(*[mask[v, dx]] * block)
+                here = scat[v] * beside(here, here)[:, : scat.shape[2]]
+                part = dot(here, scattered[j][g])
+                reach = part if reach is None else reach + part
+            for which in range(2):
+                first = 8 * g + which * block
+                part = reach[:, which * lanes : (which + 1) * lanes]
+                total[first : first + block] += part.reshape(block, wide_y, lanes)
 
     def some_views(p, carry):
         for hop in range(3, rounds):
 
-            @pl.when(p == min(hop - 3, views // width_of - 1))
+            @pl.when(p == min(hop - 3, views // 2 - 1))
             def _():
                 meet(hop)
 
-        for v in range(width_of):
-            one_view(width_of * p + v, carry)
+        two_views(p)
         return carry
 
-    lax.fori_loop(0, views // width_of, some_views, 0)
-
+    lax.fori_loop(0, views // 2, some_views, 0)
+
+    spread[0] = folded(fringe[...]).reshape(rows, cols, lanes)
+    pieces = spread_x(spread.at[0], lambda k: taps_x[k : k + 1])
+    lane = iota((cols, lanes), 1)
     for g in range(groups):
-        merged = fringe[8 * g]
-        for i in range(1, 8):
-            merged = merged + pltpu.roll(fringe[8 * g + i], 2 * rad * i, 1)
-        back_pack[g] = merged
+        turned = pieces[8 * g : 8 * g + 8]
+        step = views // 2
+        while step:
+            low_half = (lane // span) // step % 2 == 0
+            for i in range(views):
+                if i // step % 2 == 0:
+                    one, two = turned[i], turned[i + step]
+                    turned[i] = jnp.where(low_half, one, pltpu.roll(two, step * span, 1))
+                    turned[i + step] = jnp.where(low_half, pltpu.roll(one, lanes - step * span, 1), two)
+            step //= 2
+        high, low = split(stack(*turned))
+        sides = dot(mask_edge[side_of(g)], stack(high, low, high))
+        back_pack[g] = jnp.where(iota((wide_y, lanes), 1) % span < rad, sides[:wide_y], sides[wide_y:])
+    lane = iota((wide_y, lanes), 1)
     seen = jnp.zeros((8, lanes), F32)
     for dx in range(3):
         for dy in range(3):
@@ -529,7 +607,7 @@
     views = observed.shape[0]
     rad = (psf_taps.shape[2] - 1) // 2
     wide_x, wide_y = rows + 2 * rad, cols + 2 * rad
-    groups = wide_x // 8
+    groups, block = wide_x // 8, lanes // wide_y
     _, ring_a, ring_b = rings(sizes)
     n_a, n_b = len(ring_a), max(1, len(ring_b))
 
@@ -555,16 +633,21 @@
         vm(groups, wide_y, lanes),
         vm(groups, wide_y, lanes),
         vm(27, 1, lanes),
-        vm(views, 3, wide_y, 2 * lanes),
         vm(32, lanes),
+        vm(views, 3, wide_y, lanes, dtype=BF16),
+        vm(3, 2 * wide_y, 3 * lanes, dtype=BF16),
+        vm(views // 2, 2 * lanes, 2 * lanes, dtype=BF16),
+        vm(views // 2, 2 * lanes, 2 * lanes, dtype=BF16),
+        vm(views, 2 * block * cols, 2 * lanes, dtype=BF16),
+        vm(views, lanes, 3 * block * cols, dtype=BF16),
         vm(views, 2 * lanes, 2 * lanes, dtype=BF16),
         vm(views, 2 * lanes, 2 * lanes, dtype=BF16),
-        vm(views, 8 * cols, 8 * wide_y, dtype=BF16),
-        vm(views, 8 * cols, 8 * wide_y, dtype=BF16),
-        vm(views, 8 * wide_y, 16 * cols, dtype=BF16),
-        vm(wide_x, cols, lanes),
-        vm(rows, cols, lanes),
-        vm(wide_x, wide_y, lanes),
+        vm(24, lanes),
+        vm(wide_y, 3 * lanes),
+        vm(wide_x * wide_y, 2 * lanes),
+        vm(2, wide_x, cols, lanes),
+        vm(2, rows, cols, lanes),
+        vm(rows * cols, 2 * lanes),
         vm(wide_x, wide_y, lanes),
         vm(groups, wide_y, lanes),
         vm(groups, wide_y, lanes),

time: 31.5 us -> 25.5 us (0.81)
  Pallas kernels: 30.6 us -> 24.6 us
    pallas_call x1, Pallas kernels: 30.6 us -> 24.6 us  [on_device(): pl.pallas_call(functools.partial(kernel, sizes), out_shape=(jax.ShapeDtyp...]
where the time goes in v3:
time: 25.5 us; the launch traced here: 25.3 us
  Pallas kernels  24.6 us (96%)
  other arithmetic  0.67 us (3%)
    pallas_call x1, Pallas kernels, on_device(): pl.pallas_call(functools.partial(kernel, sizes), out_shape=(jax.ShapeDtyp...  24.6 us
    mul x1, other arithmetic, on_device(): return updated * factor.reshape(1, 1, lanes)  0.67 us

profile of v3, /device:TPU:0, one launch (start us, length us, event | category | flops | bytes accessed | tf_op | source)
XLA Modules:
  0.0 25.3 jit_solution(9465395732878356737)
XLA Ops:
  0.0 24.6 %shard_map.46 = (f32[16,16,128]{2,1,0:T(8,128)S(1)}, f32[1,128]{1,0:T(1,128)S(1)}) custom-call(f32[3,8,17]{2,1,0:T(8,128)} %bitcast.4, s32[8]{0:T(128)} %bitcast.5, f32[16,16,128]{2,1,0:T(8,128)} %est_hbm.1, f32[8,16,16,128]{3,2,1,0:T(8,128)} %obs_hbm.1), custom_call_target="tpu_custom_call" | custom-call | tf_op jit(solution)/shard_map/pallas_call | solution.py:665
  24.6 0.7 %broadcast_multiply_fusion = f32[16,16,128]{2,1,0:T(8,128)} fusion(f32[16,16,128]{2,1,0:T(8,128)S(1)} %get-tuple-element.7, f32[128]{0:T(128)S(1)} %bitcast.3), kind=kLoop, calls=%fused_computation | loop fusion | flops 32768 | bytes 262656 | tf_op jit(solution)/shard_map/mul | solution.py:678

commit v4 on v3

--- a/solution.py
+++ b/solution.py
@@ -37,6 +37,41 @@
         [offset for offset in offsets if offset[0] == 0],
         [offset for offset in offsets if offset[1:] == (0, 0)],
     )
+
+
+def stage_of(dx, dy, dz):
+    return 3 if dx and dy else abs(dx) + abs(dy) + abs(dz)
+
+
+def late_rounds(sizes):
+    steps = (-1, 0, 1)
+    near = [(i, j, k) for i in steps for j in steps for k in steps if (i, j, k) != (0, 0, 0)]
+    everyone = [(i, j, k) for i in range(sizes[0]) for j in range(sizes[1]) for k in range(sizes[2])]
+    known = {at: {at} for at in everyone}
+
+    def beyond(at, offset):
+        return tuple(a + b for a, b in zip(at, offset))
+
+    def heard(sets, stages):
+        return {
+            at: set().union(
+                sets[-1][at],
+                *[
+                    sets[min(stage_of(*offset), len(sets) - 1)].get(beyond(at, offset), set())
+                    for offset in near
+                    if stage_of(*offset) in stages
+                ],
+            )
+            for at in everyone
+        }
+
+    history = [known]
+    for _ in range(min(3, sum(sizes) - 3)):
+        history.append(heard([history[-1]] * 4, (1,)))
+    now, rounds = heard(history, (1, 2, 3)), 0
+    while any(len(now[at]) < len(everyone) for at in everyone):
+        now, rounds = heard([now] * 4, (1,)), rounds + 1
+    return rounds
 
 
 def kernel(
@@ -87,6 +122,9 @@
     hop_sem,
     out_send,
     out_recv,
+    far_recv,
+    weight_send,
+    weight_recv,
     back_send,
     back_recv,
     a_send,
@@ -147,7 +185,8 @@
     barrier = pltpu.get_barrier_semaphore()
     faces = [offset for offset in around if sum(map(abs, offset)) == 1]
     near_by = sum(exists(*offset).astype(jnp.int32) for offset in faces)
-    rounds = n_x + n_y + n_z - 3
+    early_rounds = min(3, n_x + n_y + n_z - 3)
+    rounds = early_rounds + late_rounds(sizes)
 
     def greet(which):
         semaphore = barrier if which == 0 else hop_sem.at[which - 1]
@@ -159,7 +198,7 @@
 
     def meet(which):
         pl.semaphore_wait(barrier if which == 0 else hop_sem.at[which - 1], near_by)
-        if which + 1 < rounds:
+        if which + 1 < rounds and which + 1 != early_rounds:
             greet(which + 1)
 
     greet(0)
@@ -199,8 +238,8 @@
         return 9 * (dz + 1) + 3 * (dx + 1) + dy + 1
 
     def out_copies(hops):
-        for dx, dy, dz in sorted(around, key=lambda offset: abs(offset[2])):
-            if sum(map(abs, (dx, dy, dz))) not in hops:
+        for dx, dy, dz in sorted(around, key=lambda offset: (abs(offset[0]), abs(offset[2]))):
+            if stage_of(dx, dy, dz) not in hops:
                 continue
             slot = slot_of(dx, dy, dz)
             size, width = (rows, rad) if dz == 0 else (pack_rows, pack_rad)
@@ -213,21 +252,24 @@
                     target.at[wide(-dx, size, width), wide(-dy, cols, rad), :],
                 ),
             )
+            sems = ((weight_send, weight_recv), (out_send, far_recv if dx else out_recv))
             copies = [
                 pltpu.make_async_remote_copy(
                     src_ref=pair[0],
                     dst_ref=pair[1],
-                    send_sem=out_send,
-                    recv_sem=out_recv,
+                    send_sem=send_sem,
+                    recv_sem=recv_sem,
                     device_id=device(dx, dy, dz),
                     device_id_type=MESH,
                 )
-                for which, pair in enumerate(pairs)
+                for pair, (send_sem, recv_sem) in zip(pairs, sems)
             ]
             yield exists(dx, dy, dz), copies
 
-    def back_copies():
-        for dx, dy, dz in sorted(around, key=lambda offset: abs(offset[2])):
+    def back_copies(flat):
+        for dx, dy, dz in around:
+            if (dz == 0) != flat:
+                continue
             size, width = (rows, rad) if dz == 0 else (pack_rows, pack_rad)
             source = total if dz == 0 else back_pack
             target = (back_right, back_xy, back_left)[dz + 1]
@@ -260,7 +302,7 @@
             device_id_type=MESH,
         ).wait_recv()
 
-    def drain_all(semaphore, extra):
+    def drain_all(semaphore, sides=(0, 1), rows_only=False):
         counts_of = [
             (min(count - 1, 2), (me > 0).astype(jnp.int32) + (me < count - 1).astype(jnp.int32))
             for me, count in ((me_x, n_x), (me_y, n_y), (me_z, n_z))
@@ -270,11 +312,14 @@
                 for c_z in range(min(1, n_z - 1), counts_of[2][0] + 1):
                     amount = 0
                     for dx, dy, dz in ((i, j, k) for i in (0, 1) for j in (0, 1) for k in (0, 1)):
-                        if (dx, dy, dz) == (0, 0, 0):
+                        if (dx, dy, dz) == (0, 0, 0) or dx not in sides:
                             continue
                         size, width = (rows, rad) if dz == 0 else (pack_rows, pack_rad)
-                        message = (width if dx else size) * (rad if dy else cols) + extra
+                        message = 1 if rows_only else (width if dx else size) * (rad if dy else cols)
                         amount += (c_x if dx else 1) * (c_y if dy else 1) * (c_z if dz else 1) * message
+
+                    if not amount:
+                        continue
 
                     @pl.when((counts_of[0][1] == c_x) & (counts_of[1][1] == c_y) & (counts_of[2][1] == c_z))
                     def _():
@@ -356,7 +401,7 @@
     stops = [min(stop, views // 2) for stop in (0, 1, 2, views // 2)]
     for hop in range(1, 4):
         lax.fori_loop(stops[hop - 1], stops[hop], build, 0)
-        if hop < min(3, rounds):
+        if hop < early_rounds:
             meet(hop)
         if hop in (1, 2):
             start(out_copies((hop + 1,)))
@@ -384,28 +429,74 @@
         count = count + weight_v
         seen = seen + weight_v * jnp.sum(obs[v].reshape(-1, 8, lanes), axis=0)
     count = count[0:1]
-    stat[0:1] = jnp.sum(seen, axis=0, keepdims=True) / count
-
-    drain_all(out_recv, 1)
-    high, low = split(ext[...].reshape(wide_x * wide_y, lanes))
-    wide_a[:, :lanes] = high
-    wide_a[:, lanes:] = low
-    wide_b[:, :lanes] = high
-    lane = iota((wide_y, lanes), 1)
-    for g in range(groups):
-        merged = jnp.where(lane % span < rad, from_left[g], from_right[g])
-        edge[g] = merged
-        high = merged.astype(BF16).astype(F32)
-        low = merged - high
-        count_of = lanes // span
-        highs = [pltpu.roll(high, span * i, 1) if i else high for i in range(count_of)]
-        lows = [pltpu.roll(low, span * i, 1) if i else low for i in range(count_of)]
-        for i in range(8):
-            third = jnp.where(lane < 2 * span, lows[(1 - i) % count_of], highs[(2 - i) % count_of])
-            terms = jnp.where(lane < span, highs[-i % count_of], third)
-            first = (8 * g + i) * wide_y
-            wide_b[first : first + wide_y, lanes:] = terms.astype(BF16)
-
+    wanted = jnp.sum(seen, axis=0, keepdims=True) / count
+
+    def side_of(g):
+        return 0 if 8 * g < rad else (1 if 8 * g < rad + rows else 2)
+
+    inner = [g for g in range(groups) if side_of(g) == 1]
+    outer = [g for g in range(groups) if side_of(g) != 1]
+    place = {g: which for which, g in enumerate(inner + outer)}
+    size = 8 * wide_y
+    inner_rows, outer_rows = slice(0, size * len(inner)), slice(size * len(inner), size * groups)
+
+    def prepare(chosen_groups):
+        lane = iota((wide_y, lanes), 1)
+        for g in chosen_groups:
+            here = slice(size * place[g], size * (place[g] + 1))
+            high, low = split(ext[8 * g : 8 * g + 8].reshape(size, lanes))
+            wide_a[here, :lanes] = high
+            wide_a[here, lanes:] = low
+            wide_b[here, :lanes] = high
+            merged = jnp.where(lane % span < rad, from_left[g], from_right[g])
+            edge[g] = merged
+            high = merged.astype(BF16).astype(F32)
+            low = merged - high
+            count_of = lanes // span
+            highs = [pltpu.roll(high, span * i, 1) if i else high for i in range(count_of)]
+            lows = [pltpu.roll(low, span * i, 1) if i else low for i in range(count_of)]
+            for i in range(8):
+                third = jnp.where(lane < 2 * span, lows[(1 - i) % count_of], highs[(2 - i) % count_of])
+                terms = jnp.where(lane < span, highs[-i % count_of], third)
+                first = size * place[g] + i * wide_y
+                wide_b[first : first + wide_y, lanes:] = terms.astype(BF16)
+
+    def spread_x(source, tap):
+        pieces = []
+        for e in range(wide_x):
+            piece = None
+            for a in range(rows):
+                if 0 <= e - a < length:
+                    term = tap(e - a) * source[a]
+                    piece = term if piece is None else piece + term
+            pieces.append(piece)
+        return pieces
+
+    def pairs_of(part, half):
+        return beside(part[:half], part[half:])
+
+    def blur_zy(p, chosen_groups, row_range, slot):
+        blurred[slot, row_range] = dot(wide_a[row_range, :], ahead_a[p]) + dot(wide_b[row_range, :], ahead_b[p])
+        for j in range(2):
+            v = 2 * p + j
+            for g in chosen_groups:
+                first = size * place[g]
+                high, low = split(blurred[slot, first : first + size, j * lanes : (j + 1) * lanes])
+                line = dot(gath[v], stack(pairs_of(high, size // 2), pairs_of(low, size // 2)))
+                half = block * cols
+                line = line[:half] + line[half:]
+                for which in range(2):
+                    first = 8 * g + which * block
+                    part = line[:, which * lanes : (which + 1) * lanes]
+                    lined[v, first : first + block] = part.reshape(block, cols, lanes)
+
+    drain_all(out_recv, sides=(0,))
+    prepare(inner)
+
+    for p in range(views // 2):
+        blur_zy(p, inner, inner_rows, p)
+
+    drain_all(weight_recv, rows_only=True)
     everyone = stack(*[weight[slot] for slot in range(27)], jnp.zeros((5, lanes), F32))
     counts = jnp.zeros(everyone.shape, F32)
 
@@ -425,46 +516,25 @@
             mask_edge[dx, side * wide_y : (side + 1) * wide_y] = terms.astype(BF16)
     inverses[...] = jnp.where(counts > 0.0, 1.0 / jnp.maximum(counts, 1.0), 0.0)
 
-    def side_of(g):
-        return 0 if 8 * g < rad else (1 if 8 * g < rad + rows else 2)
-
-    def spread_x(source, tap):
-        pieces = []
-        for e in range(wide_x):
-            piece = None
-            for a in range(rows):
-                if 0 <= e - a < length:
-                    term = tap(e - a) * source[a]
-                    piece = term if piece is None else piece + term
-            pieces.append(piece)
-        return pieces
-
-    def pairs_of(part, half):
-        return beside(part[:half], part[half:])
-
-    def two_views(p):
-        blurred[...] = dot(wide_a[...], ahead_a[p]) + dot(wide_b[...], ahead_b[p])
-        size = 8 * wide_y
+    drain_all(far_recv, sides=(1,))
+    if early_rounds < rounds:
+        greet(early_rounds)
+    prepare(outer)
+
+    def two_views(p, slot):
+        blur_zy(p, outer, outer_rows, slot)
         scattered = []
         for j in range(2):
             v = 2 * p + j
-            for g in range(groups):
-                high, low = split(blurred[g * size : (g + 1) * size, j * lanes : (j + 1) * lanes])
-                line = dot(gath[v], stack(pairs_of(high, size // 2), pairs_of(low, size // 2)))
-                half = block * cols
-                line = line[:half] + line[half:]
-                for which in range(2):
-                    first = 8 * g + which * block
-                    lined[j, first : first + block] = line[:, which * lanes : (which + 1) * lanes].reshape(block, cols, lanes)
-            blur = taps_ref[0, v, 0] * lined[j, 0:rows]
+            blur = taps_ref[0, v, 0] * lined[v, 0:rows]
             for k in range(1, length):
-                blur = blur + taps_ref[0, v, k] * lined[j, k : k + rows]
+                blur = blur + taps_ref[0, v, k] * lined[v, k : k + rows]
             ratio = (obs[v] / blur).reshape(rows * cols, lanes)
             ratio = beside(*split(ratio))
             back = folded(dot(ratio, astern[v]))
             fringe[...] += dot(ratio, astern_edge[v])
-            spread[j] = back.reshape(rows, cols, lanes)
-            pieces = spread_x(spread.at[j], lambda k: taps_ref[0, v, k])
+            spread[2 * slot + j] = back.reshape(rows, cols, lanes)
+            pieces = spread_x(spread.at[2 * slot + j], lambda k: taps_ref[0, v, k])
             sent = []
             for g in range(groups):
                 high, low = split(stack(*pieces[8 * g : 8 * g + 8]))
@@ -485,17 +555,46 @@
                 part = reach[:, which * lanes : (which + 1) * lanes]
                 total[first : first + block] += part.reshape(block, wide_y, lanes)
 
-    def some_views(p, carry):
-        for hop in range(3, rounds):
-
-            @pl.when(p == min(hop - 3, views // 2 - 1))
+    pairs = views // 2
+    at_once = 2 if pairs % 2 == 0 else 1
+    last_hops = range(early_rounds, rounds)
+
+    def some_views(t, carry):
+        for which, hop in enumerate(last_hops[:-1]):
+
+            @pl.when(t == min(which + 1, pairs // at_once - 1))
             def _():
                 meet(hop)
 
-        two_views(p)
+        for which in range(at_once):
+            two_views(at_once * t + which, which)
         return carry
 
-    lax.fori_loop(0, views // 2, some_views, 0)
+    lax.fori_loop(0, pairs // at_once, some_views, 0)
+    for hop in last_hops[-1:]:
+        meet(hop)
+    start(back_copies(True))
+    def sums_a():
+        for slot, offset in enumerate(ring_a):
+            yield pltpu.make_async_remote_copy(
+                src_ref=stat,
+                dst_ref=stat_a.at[slot],
+                send_sem=a_send,
+                recv_sem=a_recv,
+                device_id=partner(*offset),
+                device_id_type=MESH,
+            )
+
+    def sums_b():
+        for slot, offset in enumerate(ring_b):
+            yield pltpu.make_async_remote_copy(
+                src_ref=part_a,
+                dst_ref=stat_b.at[slot],
+                send_sem=b_send,
+                recv_sem=b_recv,
+                device_id=partner(*offset),
+                device_id_type=MESH,
+            )
 
     spread[0] = folded(fringe[...]).reshape(rows, cols, lanes)
     pieces = spread_x(spread.at[0], lambda k: taps_x[k : k + 1])
@@ -530,34 +629,15 @@
             part = jnp.sum(part.reshape(-1, 8, lanes), axis=0)
             left, right = (inverses[at : at + 1, :] for at in (slot - 9, slot + 9))
             seen = seen + part * jnp.where(lane[0:1] % (2 * rad) < rad, left, right)
-    stat[1:2] = jnp.sum(seen, axis=0, keepdims=True)
-
-    def sums_a():
-        for slot, offset in enumerate(ring_a):
-            yield pltpu.make_async_remote_copy(
-                src_ref=stat,
-                dst_ref=stat_a.at[slot],
-                send_sem=a_send,
-                recv_sem=a_recv,
-                device_id=partner(*offset),
-                device_id_type=MESH,
-            )
-
-    def sums_b():
-        for slot, offset in enumerate(ring_b):
-            yield pltpu.make_async_remote_copy(
-                src_ref=part_a,
-                dst_ref=stat_b.at[slot],
-                send_sem=b_send,
-                recv_sem=b_recv,
-                device_id=partner(*offset),
-                device_id_type=MESH,
-            )
+    wanted = wanted + pltpu.roll(wanted, lanes // 2, 1)
+    gotten = jnp.sum(seen, axis=0, keepdims=True)
+    gotten = gotten + pltpu.roll(gotten, lanes // 2, 1)
+    stat[...] = jnp.where(iota((1, lanes), 1) < lanes // 2, wanted, gotten)
 
     for copy in sums_a():
         copy.start()
-    start(back_copies())
-    drain_all(back_recv, 0)
+    start(back_copies(False))
+    drain_all(back_recv)
     near = back_xy[...]
 
     def fold(values, size, rad, axis):
@@ -582,24 +662,26 @@
         updated = ext[rad + x, own_y, :] * (summed / count)
         out_ref[x] = updated
 
-    drain(a_recv, 2 * len(ring_a))
+    drain(a_recv, len(ring_a))
     everything = stat[...] + jnp.sum(stat_a[...], axis=0)
     if ring_b:
         part_a[...] = everything
         for copy in sums_b():
             copy.start()
-        drain(b_recv, 2 * len(ring_b))
+        drain(b_recv, len(ring_b))
         everything = part_a[...] + jnp.sum(stat_b[...], axis=0)
-    wanted = jnp.sum(everything[0:1], axis=1, keepdims=True)
-    gotten = jnp.sum(everything[1:2], axis=1, keepdims=True)
+    first_half = iota((1, lanes), 1) < lanes // 2
+    wanted = jnp.sum(jnp.where(first_half, everything, 0.0), axis=1, keepdims=True)
+    gotten = jnp.sum(jnp.where(first_half, 0.0, everything), axis=1, keepdims=True)
     factor = jnp.broadcast_to(wanted, (1, lanes)) / jnp.broadcast_to(gotten, (1, lanes))
     factor_ref[...] = factor
 
-    drain_all(out_send, 1)
-    drain_all(back_send, 0)
-    drain(a_send, 2 * len(ring_a))
+    drain_all(out_send)
+    drain_all(weight_send, rows_only=True)
+    drain_all(back_send)
+    drain(a_send, len(ring_a))
     if ring_b:
-        drain(b_send, 2 * len(ring_b))
+        drain(b_send, len(ring_b))
 
 
 def on_device(sizes, estimate, observed, coverage, psf_taps):
@@ -644,23 +726,23 @@
         vm(views, 2 * lanes, 2 * lanes, dtype=BF16),
         vm(24, lanes),
         vm(wide_y, 3 * lanes),
-        vm(wide_x * wide_y, 2 * lanes),
-        vm(2, wide_x, cols, lanes),
-        vm(2, rows, cols, lanes),
+        vm(views // 2, wide_x * wide_y, 2 * lanes),
+        vm(views, wide_x, cols, lanes),
+        vm(views, rows, cols, lanes),
         vm(rows * cols, 2 * lanes),
         vm(wide_x, wide_y, lanes),
         vm(groups, wide_y, lanes),
         vm(groups, wide_y, lanes),
         vm(groups, wide_y, lanes),
         vm(wide_x, wide_y, lanes),
-        vm(2, lanes),
-        vm(n_a, 2, lanes),
-        vm(n_b, 2, lanes),
-        vm(2, lanes),
+        vm(1, lanes),
+        vm(n_a, 1, lanes),
+        vm(n_b, 1, lanes),
+        vm(1, lanes),
         vm(5 * rows * cols, 1, lanes),
         dma(4),
-        pltpu.SemaphoreType.REGULAR((max(1, sum(sizes) - 4),)),
-        *[pltpu.SemaphoreType.DMA] * 8,
+        pltpu.SemaphoreType.REGULAR((max(1, min(3, sum(sizes) - 3) + late_rounds(sizes)),)),
+        *[pltpu.SemaphoreType.DMA] * 11,
     ]
     updated, factor = pl.pallas_call(
         functools.partial(kernel, sizes),

time: 25.5 us -> 24.7 us (0.969)
  Pallas kernels: 24.6 us -> 23.9 us
    pallas_call x1, Pallas kernels: 24.6 us -> 23.9 us  [on_device(): pl.pallas_call(functools.partial(kernel, sizes), out_shape=(jax.ShapeDtyp...]
where the time goes in v4:
time: 24.7 us; the launch traced here: 24.5 us
  Pallas kernels  23.9 us (97%)
  other arithmetic  0.67 us (3%)
    pallas_call x1, Pallas kernels, on_device(): pl.pallas_call(functools.partial(kernel, sizes), out_shape=(jax.ShapeDtyp...  23.9 us
    mul x1, other arithmetic, on_device(): return updated * factor.reshape(1, 1, lanes)  0.67 us

profile of v4, /device:TPU:0, one launch (start us, length us, event | category | flops | bytes accessed | tf_op | source)
XLA Modules:
  0.0 24.5 jit_solution(15251518301173018697)
XLA Ops:
  0.0 23.9 %shard_map.46 = (f32[16,16,128]{2,1,0:T(8,128)S(1)}, f32[1,128]{1,0:T(1,128)S(1)}) custom-call(f32[3,8,17]{2,1,0:T(8,128)} %bitcast.4, s32[8]{0:T(128)} %bitcast.5, f32[16,16,128]{2,1,0:T(8,128)} %est_hbm.1, f32[8,16,16,128]{3,2,1,0:T(8,128)} %obs_hbm.1), custom_call_target="tpu_custom_call" | custom-call | tf_op jit(solution)/shard_map/pallas_call | solution.py:747
  23.9 0.7 %broadcast_multiply_fusion = f32[16,16,128]{2,1,0:T(8,128)} fusion(f32[16,16,128]{2,1,0:T(8,128)S(1)} %get-tuple-element.7, f32[128]{0:T(128)S(1)} %bitcast.3), kind=kLoop, calls=%fused_computation | loop fusion | flops 32768 | bytes 262656 | tf_op jit(solution)/shard_map/mul | solution.py:760

commit v5 on v4

--- a/solution.py
+++ b/solution.py
@@ -37,6 +37,9 @@
         [offset for offset in offsets if offset[0] == 0],
         [offset for offset in offsets if offset[1:] == (0, 0)],
     )
+
+
+EARLY = 5
 
 
 def stage_of(dx, dy, dz):
@@ -66,12 +69,16 @@
         }
 
     history = [known]
-    for _ in range(min(3, sum(sizes) - 3)):
+    for _ in range(min(EARLY, sum(sizes) - 3)):
         history.append(heard([history[-1]] * 4, (1,)))
     now, rounds = heard(history, (1, 2, 3)), 0
     while any(len(now[at]) < len(everyone) for at in everyone):
         now, rounds = heard([now] * 4, (1,)), rounds + 1
     return rounds
+
+
+def extent_y(n_y, cols, rad):
+    return cols + (rad if n_y == 2 else 2 * rad)
 
 
 def kernel(
@@ -136,11 +143,15 @@
     views, rows, cols, lanes = obs.shape
     length = taps_ref.shape[2]
     rad = (length - 1) // 2
-    wide_x, wide_y = rows + 2 * rad, cols + 2 * rad
+    wide_x, wide_y = rows + 2 * rad, extent_y(n_y, cols, rad)
     groups = wide_x // 8
+    first_y = wide_y - cols - rad
+    bands_y = [(first_y, cols, 1), (first_y + cols, rad, 2)]
+    if first_y:
+        bands_y.insert(0, (0, rad, 0))
     me_x, me_y, me_z = lax.axis_index("bx"), lax.axis_index("by"), lax.axis_index("bz")
 
-    own_x, own_y = slice(rad, rad + rows), slice(rad, rad + cols)
+    own_x, own_y = slice(rad, rad + rows), slice(first_y, first_y + cols)
     own = ext.at[own_x, own_y, :]
     loads = [
         pltpu.make_async_copy(source, target, fetch_sem.at[which])
@@ -176,8 +187,9 @@
 
     for part in ((slice(0, rad), slice(0, wide_y)), (slice(rad + rows, wide_x), slice(0, wide_y))):
         ext[part[0], part[1], :] = jnp.zeros((rad, wide_y, lanes), F32)
-    for part in (slice(0, rad), slice(rad + cols, wide_y)):
-        ext[own_x, part, :] = jnp.zeros((rows, rad, lanes), F32)
+    for start_y, size_y, dy in bands_y:
+        if dy != 1:
+            ext[own_x, start_y : start_y + size_y, :] = jnp.zeros((rows, size_y, lanes), F32)
     from_left[...] = jnp.zeros(from_left.shape, F32)
     from_right[...] = jnp.zeros(from_right.shape, F32)
     weight[...] = jnp.zeros(weight.shape, F32)
@@ -185,7 +197,7 @@
     barrier = pltpu.get_barrier_semaphore()
     faces = [offset for offset in around if sum(map(abs, offset)) == 1]
     near_by = sum(exists(*offset).astype(jnp.int32) for offset in faces)
-    early_rounds = min(3, n_x + n_y + n_z - 3)
+    early_rounds = min(EARLY, n_x + n_y + n_z - 3)
     rounds = early_rounds + late_rounds(sizes)
 
     def greet(which):
@@ -218,53 +230,50 @@
     weight[13] = row
     loads[0].wait()
 
-    lane = lax.broadcasted_iota(jnp.int32, (cols, lanes), 1)
-    for g in range(rows // 8):
-        merged = jnp.zeros((cols, lanes), F32)
-        for i in range(8):
-            rolled = pltpu.roll(ext[rad + 8 * g + i, own_y, :], 2 * rad * i + rad, 1)
-            merged = jnp.where(lane // (2 * rad) == i, rolled, merged)
-        pack[g] = merged
-
     def cut(step, size, width):
         return pl.ds(0, size) if step == 0 else pl.ds(0 if step < 0 else size - width, width)
 
     def wide(step, size, width):
         return pl.ds(width, size) if step == 0 else pl.ds(0 if step < 0 else width + size, width)
 
+    def wide_cols(step):
+        if step == 0:
+            return pl.ds(first_y, cols)
+        return pl.ds(0 if step < 0 and first_y else first_y + cols, rad)
+
+    def place_y(row):
+        return row - first_y if first_y else jnp.where(row < cols, row, row - me_y * wide_y)
+
     pack_rows, pack_rad = rows // 8, rad // 8
 
     def slot_of(dx, dy, dz):
         return 9 * (dz + 1) + 3 * (dx + 1) + dy + 1
 
-    def out_copies(hops):
+    def out_copies(hops, what, flat=(True, False)):
         for dx, dy, dz in sorted(around, key=lambda offset: (abs(offset[0]), abs(offset[2]))):
-            if stage_of(dx, dy, dz) not in hops:
+            if stage_of(dx, dy, dz) not in hops or (dz == 0) not in flat:
                 continue
             slot = slot_of(dx, dy, dz)
             size, width = (rows, rad) if dz == 0 else (pack_rows, pack_rad)
             source = own if dz == 0 else pack
             target = (from_right, ext, from_left)[dz + 1]
             pairs = (
-                (weight.at[13], weight.at[slot_of(-dx, -dy, -dz)]),
+                (weight.at[13], weight.at[slot_of(-dx, -dy if first_y else abs(dy), -dz)]),
                 (
                     source.at[cut(dx, size, width), cut(dy, cols, rad), :],
-                    target.at[wide(-dx, size, width), wide(-dy, cols, rad), :],
+                    target.at[wide(-dx, size, width), wide_cols(-dy), :],
                 ),
             )
             sems = ((weight_send, weight_recv), (out_send, far_recv if dx else out_recv))
-            copies = [
-                pltpu.make_async_remote_copy(
-                    src_ref=pair[0],
-                    dst_ref=pair[1],
-                    send_sem=send_sem,
-                    recv_sem=recv_sem,
-                    device_id=device(dx, dy, dz),
-                    device_id_type=MESH,
-                )
-                for pair, (send_sem, recv_sem) in zip(pairs, sems)
-            ]
-            yield exists(dx, dy, dz), copies
+            copy = pltpu.make_async_remote_copy(
+                src_ref=pairs[what][0],
+                dst_ref=pairs[what][1],
+                send_sem=sems[what][0],
+                recv_sem=sems[what][1],
+                device_id=device(dx, dy, dz),
+                device_id_type=MESH,
+            )
+            yield exists(dx, dy, dz), [copy]
 
     def back_copies(flat):
         for dx, dy, dz in around:
@@ -274,8 +283,8 @@
             source = total if dz == 0 else back_pack
             target = (back_right, back_xy, back_left)[dz + 1]
             copy = pltpu.make_async_remote_copy(
-                src_ref=source.at[wide(dx, size, width), wide(dy, cols, rad), :],
-                dst_ref=target.at[wide(-dx, size, width), wide(-dy, cols, rad), :],
+                src_ref=source.at[wide(dx, size, width), wide_cols(dy), :],
+                dst_ref=target.at[wide(-dx, size, width), wide_cols(-dy), :],
                 send_sem=back_send,
                 recv_sem=back_recv,
                 device_id=device(dx, dy, dz),
@@ -329,7 +338,8 @@
         return lax.broadcasted_iota(jnp.int32, shape, dim)
 
     span = 2 * rad
-    block = lanes // wide_y
+    block = lanes // (cols + 2 * rad)
+    part_rows = block * wide_y
 
     def stack(*parts):
         return jnp.concatenate(parts, axis=0)
@@ -375,11 +385,12 @@
             astern_edge[v] = stack(beside(high, low), beside(high, jnp.zeros(square, BF16)))
             shape = (block * cols, lanes)
             row, col = iota(shape, 0), iota(shape, 1)
-            offset = jnp.where(row // cols == col // wide_y, col % wide_y - row % cols, -1)
+            offset = jnp.where(row // cols == col // wide_y, place_y(col % wide_y) + rad - row % cols, -1)
             blur_y = chosen(offset, 1)
             high, low = split(blur_y)
-            gath[v] = stack(beside(high, high), beside(low, jnp.zeros(shape, BF16)))
-            turned = blur_y.T
+            high, low = high[:, :part_rows], low[:, :part_rows]
+            gath[v] = stack(beside(high, high), beside(low, jnp.zeros(low.shape, BF16)))
+            turned = blur_y.T[:part_rows]
             high = turned.astype(BF16).astype(F32)
             low = turned - high
             scat[v] = beside(high, high, low).astype(BF16)
@@ -396,20 +407,31 @@
         return lines
 
     meet(0)
-    start(out_copies((1,)))
+    start(out_copies((1,), 1, (True,)))
+    lane = lax.broadcasted_iota(jnp.int32, (cols, lanes), 1)
+    for g in range(rows // 8):
+        merged = jnp.zeros((cols, lanes), F32)
+        for i in range(8):
+            rolled = pltpu.roll(ext[rad + 8 * g + i, own_y, :], 2 * rad * i + rad, 1)
+            merged = jnp.where(lane // (2 * rad) == i, rolled, merged)
+        pack[g] = merged
+
+    start(out_copies((1,), 0))
+    start(out_copies((1,), 1, (False,)))
     loads[2].wait()
     stops = [min(stop, views // 2) for stop in (0, 1, 2, views // 2)]
     for hop in range(1, 4):
         lax.fori_loop(stops[hop - 1], stops[hop], build, 0)
-        if hop < early_rounds:
+        if hop < min(3, early_rounds):
             meet(hop)
         if hop in (1, 2):
-            start(out_copies((hop + 1,)))
+            start(out_copies((hop + 1,), 0))
+            start(out_copies((hop + 1,), 1))
 
     for k, line in enumerate(lines_of(0)):
         taps_x[k : k + 1] = line
     shape = (wide_y, lanes)
-    offset = iota(shape, 0) - iota(shape, 1) % cols
+    offset = place_y(iota(shape, 0)) + rad - iota(shape, 1) % cols
     base = jnp.zeros(shape, F32)
     for k, line in enumerate(lines_of(1)):
         base = jnp.where(offset == k, line, base)
@@ -455,11 +477,12 @@
             count_of = lanes // span
             highs = [pltpu.roll(high, span * i, 1) if i else high for i in range(count_of)]
             lows = [pltpu.roll(low, span * i, 1) if i else low for i in range(count_of)]
+            rows_of = []
             for i in range(8):
                 third = jnp.where(lane < 2 * span, lows[(1 - i) % count_of], highs[(2 - i) % count_of])
                 terms = jnp.where(lane < span, highs[-i % count_of], third)
-                first = size * place[g] + i * wide_y
-                wide_b[first : first + wide_y, lanes:] = terms.astype(BF16)
+                rows_of.append(terms)
+            wide_b[here, lanes:] = stack(*rows_of).astype(BF16)
 
     def spread_x(source, tap):
         pieces = []
@@ -491,29 +514,33 @@
                     lined[v, first : first + block] = part.reshape(block, cols, lanes)
 
     drain_all(out_recv, sides=(0,))
+    if early_rounds > 3:
+        meet(3)
     prepare(inner)
 
     for p in range(views // 2):
         blur_zy(p, inner, inner_rows, p)
 
+    for hop in range(4, early_rounds):
+        meet(hop)
     drain_all(weight_recv, rows_only=True)
     everyone = stack(*[weight[slot] for slot in range(27)], jnp.zeros((5, lanes), F32))
     counts = jnp.zeros(everyone.shape, F32)
 
     def along_y(rows_of, first):
-        bands = [(rad, 0), (cols, 1), (rad, 2)]
-        return stack(*[jnp.broadcast_to(rows_of[first + dy : first + dy + 1], (size, lanes)) for size, dy in bands])
+        return stack(*[jnp.broadcast_to(rows_of[first + dy : first + dy + 1], (size_y, lanes)) for _, size_y, dy in bands_y])
 
     for v in range(views):
         theirs = weight_of(everyone, v)
         counts = counts + theirs
         for dx in range(3):
-            mask[v, dx] = along_y(theirs, 9 + 3 * dx).astype(BF16)
+            mask[v, dx] = stack(*[along_y(theirs, 9 + 3 * dx)] * block).astype(BF16)
     for dx in range(3):
+        terms = []
         for side in range(2):
             part = along_y(everyone, 18 * side + 3 * dx)
-            terms = scat_edge[...] * beside(part, part, part)
-            mask_edge[dx, side * wide_y : (side + 1) * wide_y] = terms.astype(BF16)
+            terms.append(scat_edge[...] * beside(part, part, part))
+        mask_edge[dx] = stack(*terms).astype(BF16)
     inverses[...] = jnp.where(counts > 0.0, 1.0 / jnp.maximum(counts, 1.0), 0.0)
 
     drain_all(far_recv, sides=(1,))
@@ -546,7 +573,7 @@
             reach = None
             for j in range(2):
                 v = 2 * p + j
-                here = stack(*[mask[v, dx]] * block)
+                here = mask[v, dx]
                 here = scat[v] * beside(here, here)[:, : scat.shape[2]]
                 part = dot(here, scattered[j][g])
                 reach = part if reach is None else reach + part
@@ -555,23 +582,9 @@
                 part = reach[:, which * lanes : (which + 1) * lanes]
                 total[first : first + block] += part.reshape(block, wide_y, lanes)
 
-    pairs = views // 2
-    at_once = 2 if pairs % 2 == 0 else 1
-    last_hops = range(early_rounds, rounds)
-
-    def some_views(t, carry):
-        for which, hop in enumerate(last_hops[:-1]):
-
-            @pl.when(t == min(which + 1, pairs // at_once - 1))
-            def _():
-                meet(hop)
-
-        for which in range(at_once):
-            two_views(at_once * t + which, which)
-        return carry
-
-    lax.fori_loop(0, pairs // at_once, some_views, 0)
-    for hop in last_hops[-1:]:
+    for p in range(views // 2):
+        two_views(p, p)
+    for hop in range(early_rounds, rounds):
         meet(hop)
     start(back_copies(True))
     def sums_a():
@@ -616,10 +629,9 @@
     lane = iota((wide_y, lanes), 1)
     seen = jnp.zeros((8, lanes), F32)
     for dx in range(3):
-        for dy in range(3):
-            first_y, last_y = ((0, rad), (rad, rad + cols), (rad + cols, wide_y))[dy]
+        for start_y, size_y, dy in bands_y:
             first_x, last_x = ((0, rad), (rad, rad + rows), (rad + rows, wide_x))[dx]
-            part_y = slice(first_y, last_y)
+            part_y = slice(start_y, start_y + size_y)
             part = total[first_x:last_x, part_y, :] * ext[first_x:last_x, part_y, :]
             part = jnp.sum(part.reshape(-1, 8, lanes), axis=0)
             slot = 9 + 3 * dx + dy
@@ -651,14 +663,22 @@
         gap = jnp.zeros(gap_shape, F32)
         return mid + jnp.concatenate([low, gap], axis=axis) + jnp.concatenate([gap, top], axis=axis)
 
-    near = fold(fold(near, rows, rad, 0), cols, rad, 1)
+    def fold_y(values):
+        if first_y:
+            return fold(values, cols, rad, 1)
+        part = values[:, cols:]
+        gap = jnp.zeros((part.shape[0], cols - rad, lanes), F32)
+        before, after = (jnp.concatenate(pair, axis=1) for pair in ((part, gap), (gap, part)))
+        return values[:, :cols] + jnp.where(me_y == 0, after, before)
+
+    near = fold_y(fold(near, rows, rad, 0))
     ends = jnp.where((lane % (2 * rad) < rad)[None], back_right[...], back_left[...])
-    ends = fold(fold(ends, pack_rows, pack_rad, 0), cols, rad, 1)
+    ends = fold_y(fold(ends, pack_rows, pack_rad, 0))
     lane = lax.broadcasted_iota(jnp.int32, (cols, lanes), 1)
     outer = (lane < rad) | (lane >= lanes - rad)
     for x in range(rows):
         rolled = pltpu.roll(ends[x // 8], lanes - (2 * rad * (x % 8) + rad), 1)
-        summed = total[rad + x, rad : rad + cols, :] + near[x] + jnp.where(outer, rolled, 0.0)
+        summed = total[rad + x, own_y, :] + near[x] + jnp.where(outer, rolled, 0.0)
         updated = ext[rad + x, own_y, :] * (summed / count)
         out_ref[x] = updated
 
@@ -688,8 +708,8 @@
     rows, cols, lanes = estimate.shape
     views = observed.shape[0]
     rad = (psf_taps.shape[2] - 1) // 2
-    wide_x, wide_y = rows + 2 * rad, cols + 2 * rad
-    groups, block = wide_x // 8, lanes // wide_y
+    wide_x, wide_y = rows + 2 * rad, extent_y(sizes[1], cols, rad)
+    groups, block = wide_x // 8, lanes // (cols + 2 * rad)
     _, ring_a, ring_b = rings(sizes)
     n_a, n_b = len(ring_a), max(1, len(ring_b))
 
@@ -716,12 +736,12 @@
         vm(groups, wide_y, lanes),
         vm(27, 1, lanes),
         vm(32, lanes),
-        vm(views, 3, wide_y, lanes, dtype=BF16),
+        vm(views, 3, block * wide_y, lanes, dtype=BF16),
         vm(3, 2 * wide_y, 3 * lanes, dtype=BF16),
         vm(views // 2, 2 * lanes, 2 * lanes, dtype=BF16),
         vm(views // 2, 2 * lanes, 2 * lanes, dtype=BF16),
-        vm(views, 2 * block * cols, 2 * lanes, dtype=BF16),
-        vm(views, lanes, 3 * block * cols, dtype=BF16),
+        vm(views, 2 * block * cols, 2 * block * wide_y, dtype=BF16),
+        vm(views, block * wide_y, 3 * block * cols, dtype=BF16),
         vm(views, 2 * lanes, 2 * lanes, dtype=BF16),
         vm(views, 2 * lanes, 2 * lanes, dtype=BF16),
         vm(24, lanes),
@@ -741,7 +761,7 @@
         vm(1, lanes),
         vm(5 * rows * cols, 1, lanes),
         dma(4),
-        pltpu.SemaphoreType.REGULAR((max(1, min(3, sum(sizes) - 3) + late_rounds(sizes)),)),
+        pltpu.SemaphoreType.REGULAR((max(1, min(EARLY, sum(sizes) - 3) + late_rounds(sizes)),)),
         *[pltpu.SemaphoreType.DMA] * 11,
     ]
     updated, factor = pl.pallas_call(

time: 24.7 us -> 23.4 us (0.947)
  Pallas kernels: 23.9 us -> 22.6 us
    pallas_call x1, Pallas kernels: 23.9 us -> 22.6 us  [on_device(): pl.pallas_call(functools.partial(kernel, sizes), out_shape=(jax.ShapeDtyp...]
where the time goes in v5:
time: 23.4 us; the launch traced here: 23.3 us
  Pallas kernels  22.6 us (97%)
  other arithmetic  0.67 us (3%)
    pallas_call x1, Pallas kernels, on_device(): pl.pallas_call(functools.partial(kernel, sizes), out_shape=(jax.ShapeDtyp...  22.6 us
    mul x1, other arithmetic, on_device(): return updated * factor.reshape(1, 1, lanes)  0.67 us

profile of v5, /device:TPU:0, one launch (start us, length us, event | category | flops | bytes accessed | tf_op | source)
XLA Modules:
  0.0 23.3 jit_solution(1562109991181329420)
XLA Ops:
  0.0 22.6 %shard_map.46 = (f32[16,16,128]{2,1,0:T(8,128)S(1)}, f32[1,128]{1,0:T(1,128)S(1)}) custom-call(f32[3,8,17]{2,1,0:T(8,128)} %bitcast.4, s32[8]{0:T(128)} %bitcast.5, f32[16,16,128]{2,1,0:T(8,128)} %est_hbm.1, f32[8,16,16,128]{3,2,1,0:T(8,128)} %obs_hbm.1), custom_call_target="tpu_custom_call" | custom-call | tf_op jit(solution)/shard_map/pallas_call | solution.py:767
  22.6 0.7 %broadcast_multiply_fusion = f32[16,16,128]{2,1,0:T(8,128)} fusion(f32[16,16,128]{2,1,0:T(8,128)S(1)} %get-tuple-element.7, f32[128]{0:T(128)S(1)} %bitcast.3), kind=kLoop, calls=%fused_computation | loop fusion | flops 32768 | bytes 262656 | tf_op jit(solution)/shard_map/mul | solution.py:780

commit v6 on v5

--- a/solution.py
+++ b/solution.py
@@ -250,7 +250,7 @@
         return 9 * (dz + 1) + 3 * (dx + 1) + dy + 1
 
     def out_copies(hops, what, flat=(True, False)):
-        for dx, dy, dz in sorted(around, key=lambda offset: (abs(offset[0]), abs(offset[2]))):
+        for dx, dy, dz in sorted(around, key=lambda offset: (abs(offset[0]), abs(offset[2]) if stage_of(*offset) < 3 else -abs(offset[2]))):
             if stage_of(dx, dy, dz) not in hops or (dz == 0) not in flat:
                 continue
             slot = slot_of(dx, dy, dz)
@@ -276,7 +276,7 @@
             yield exists(dx, dy, dz), [copy]
 
     def back_copies(flat):
-        for dx, dy, dz in around:
+        for dx, dy, dz in sorted(around, key=lambda offset: -sum(map(abs, offset))):
             if (dz == 0) != flat:
                 continue
             size, width = (rows, rad) if dz == 0 else (pack_rows, pack_rad)
@@ -484,16 +484,59 @@
                 rows_of.append(terms)
             wide_b[here, lanes:] = stack(*rows_of).astype(BF16)
 
+    def weighed(terms):
+        result = None
+        for factor, value in terms:
+            term = factor * value
+            result = term if result is None else result + term
+        return result
+
+    def added(one, two):
+        if one is None or two is None:
+            return two if one is None else one
+        return one + two
+
+    def blur_x(source, tap):
+        taps = [tap(k) for k in range(length)]
+        even, odd = taps[0::2], [None] + taps[1::2]
+        both = [added(one, two) for one, two in zip(even, odd)]
+        reach, columns = len(even), []
+        for first in range(0, cols, 8):
+            values = [source[e, first : first + 8, :] for e in range(wide_x)]
+            left, right = values[0::2], values[1::2]
+            joined = [one + two for one, two in zip(left, right)]
+            lines, before = [], weighed([(odd[j], right[j - 1]) for j in range(1, reach)])
+            for m in range(rows // 2):
+                one = weighed([(even[j], left[m + j]) for j in range(reach)])
+                two = weighed([(odd[j], right[m + j]) for j in range(1, reach)])
+                three = weighed([(both[j], joined[m + j]) for j in range(reach)])
+                lines += [one + before, three - (one + two)]
+                before = two
+            columns.append(lines)
+        return [stack(*parts) for parts in zip(*columns)]
+
     def spread_x(source, tap):
-        pieces = []
-        for e in range(wide_x):
-            piece = None
-            for a in range(rows):
-                if 0 <= e - a < length:
-                    term = tap(e - a) * source[a]
-                    piece = term if piece is None else piece + term
-            pieces.append(piece)
-        return pieces
+        taps = [tap(k) for k in range(length)]
+        even, odd = taps[0::2], taps[1::2] + [None]
+        both = [added(one, two) for one, two in zip(even, odd)]
+        columns = []
+        for first in range(0, cols, 8):
+            values = [source[a, first : first + 8, :] for a in range(rows)]
+            left, right = values[0::2], values[1::2]
+            joined = [one + two for one, two in zip(left, right)]
+
+            def product(factors, parts, n):
+                pairs = [(factors[n - i], parts[i]) for i in range(len(parts)) if 0 <= n - i < len(factors)]
+                return weighed([pair for pair in pairs if pair[0] is not None])
+
+            lines, before = [], None
+            for n in range(wide_x // 2):
+                one, two = product(even, left, n), product(odd, right, n)
+                three = product(both, joined, n)
+                lines += [added(one, before), three - added(one, two)]
+                before = two
+            columns.append(lines)
+        return [stack(*parts) for parts in zip(*columns)]
 
     def pairs_of(part, half):
         return beside(part[:half], part[half:])
@@ -553,10 +596,8 @@
         scattered = []
         for j in range(2):
             v = 2 * p + j
-            blur = taps_ref[0, v, 0] * lined[v, 0:rows]
-            for k in range(1, length):
-                blur = blur + taps_ref[0, v, k] * lined[v, k : k + rows]
-            ratio = (obs[v] / blur).reshape(rows * cols, lanes)
+            blur = blur_x(lined.at[v], lambda k: taps_ref[0, v, k])
+            ratio = obs[v].reshape(rows * cols, lanes) / stack(*blur)
             ratio = beside(*split(ratio))
             back = folded(dot(ratio, astern[v]))
             fringe[...] += dot(ratio, astern_edge[v])

time: 23.4 us -> 23 us (0.983)
  Pallas kernels: 22.6 us -> 22.2 us
    pallas_call x1, Pallas kernels: 22.6 us -> 22.2 us  [on_device(): pl.pallas_call(functools.partial(kernel, sizes), out_shape=(jax.ShapeDtyp...]
where the time goes in v6:
time: 23 us; the launch traced here: 22.9 us
  Pallas kernels  22.2 us (97%)
  other arithmetic  0.67 us (3%)
    pallas_call x1, Pallas kernels, on_device(): pl.pallas_call(functools.partial(kernel, sizes), out_shape=(jax.ShapeDtyp...  22.2 us
    mul x1, other arithmetic, on_device(): return updated * factor.reshape(1, 1, lanes)  0.67 us

profile of v6, /device:TPU:0, one launch (start us, length us, event | category | flops | bytes accessed | tf_op | source)
XLA Modules:
  0.0 22.9 jit_solution(13422166906143987679)
XLA Ops:
  0.0 22.2 %shard_map.46 = (f32[16,16,128]{2,1,0:T(8,128)S(1)}, f32[1,128]{1,0:T(1,128)S(1)}) custom-call(f32[3,8,17]{2,1,0:T(8,128)} %bitcast.4, s32[8]{0:T(128)} %bitcast.5, f32[16,16,128]{2,1,0:T(8,128)} %est_hbm.1, f32[8,16,16,128]{3,2,1,0:T(8,128)} %obs_hbm.1), custom_call_target="tpu_custom_call" | custom-call | tf_op jit(solution)/shard_map/pallas_call | solution.py:808
  22.2 0.7 %broadcast_multiply_fusion = f32[16,16,128]{2,1,0:T(8,128)} fusion(f32[16,16,128]{2,1,0:T(8,128)S(1)} %get-tuple-element.7, f32[128]{0:T(128)S(1)} %bitcast.3), kind=kLoop, calls=%fused_computation | loop fusion | flops 32768 | bytes 262656 | tf_op jit(solution)/shard_map/mul | solution.py:821

commit v7 on v6

--- a/solution.py
+++ b/solution.py
@@ -567,6 +567,9 @@
     for hop in range(4, early_rounds):
         meet(hop)
     drain_all(weight_recv, rows_only=True)
+    drain_all(far_recv, sides=(1,))
+    if early_rounds < rounds:
+        greet(early_rounds)
     everyone = stack(*[weight[slot] for slot in range(27)], jnp.zeros((5, lanes), F32))
     counts = jnp.zeros(everyone.shape, F32)
 
@@ -586,9 +589,6 @@
         mask_edge[dx] = stack(*terms).astype(BF16)
     inverses[...] = jnp.where(counts > 0.0, 1.0 / jnp.maximum(counts, 1.0), 0.0)
 
-    drain_all(far_recv, sides=(1,))
-    if early_rounds < rounds:
-        greet(early_rounds)
     prepare(outer)
 
     def two_views(p, slot):

time: 23 us -> 22.9 us (level)
  no operation moved by 1% of the time
where the time goes in v7:
time: 22.9 us; the launch traced here: 22.8 us
  Pallas kernels  22.1 us (97%)
  other arithmetic  0.67 us (3%)
    pallas_call x1, Pallas kernels, on_device(): pl.pallas_call(functools.partial(kernel, sizes), out_shape=(jax.ShapeDtyp...  22.1 us
    mul x1, other arithmetic, on_device(): return updated * factor.reshape(1, 1, lanes)  0.67 us

profile of v7, /device:TPU:0, one launch (start us, length us, event | category | flops | bytes accessed | tf_op | source)
XLA Modules:
  0.0 22.8 jit_solution(17349624410943318053)
XLA Ops:
  0.0 22.1 %shard_map.46 = (f32[16,16,128]{2,1,0:T(8,128)S(1)}, f32[1,128]{1,0:T(1,128)S(1)}) custom-call(f32[3,8,17]{2,1,0:T(8,128)} %bitcast.4, s32[8]{0:T(128)} %bitcast.5, f32[16,16,128]{2,1,0:T(8,128)} %est_hbm.1, f32[8,16,16,128]{3,2,1,0:T(8,128)} %obs_hbm.1), custom_call_target="tpu_custom_call" | custom-call | tf_op jit(solution)/shard_map/pallas_call | solution.py:808
  22.1 0.7 %broadcast_multiply_fusion = f32[16,16,128]{2,1,0:T(8,128)} fusion(f32[16,16,128]{2,1,0:T(8,128)S(1)} %get-tuple-element.7, f32[128]{0:T(128)S(1)} %bitcast.3), kind=kLoop, calls=%fused_computation | loop fusion | flops 32768 | bytes 262656 | tf_op jit(solution)/shard_map/mul | solution.py:821
